TPU v7x, 32 devices: a whole 2x2x4 slice. The times are simulated.
32 devices in a mesh: member: 8 (over y, x, core), region: 4 (over z).
Axes of the slice: x: 2, y: 2, z: 4, core: 2. Of those that a mesh axis runs over, the one named last changes fastest.
Arguments:
- prior_sample_matrix: float32 [128, 65536], P(('member', 'region')), may hold values from -18 to 18
- obs_values: float32 [1024], replicated, may hold values from -18 to 18
- obs_var: float32 [1024], replicated, may hold values from 0.5 to 4
- measured_indexes: int32 [1024], replicated, may hold values from 0 to 65535
- neighbours: int32 [128, 128], replicated, may hold values from 0 to 1023, as said below
- perturbation: float32 [128, 1024], P(('member', 'region')), may hold values from -6 to 6
- counts: int32 [32], replicated, may hold values from 1 to 8, as said below
Outputs:
- owned: float32 [256, 65536], P(('member', 'region'))
Inputs may be any that keep to these rules, and one draw needn't show every extreme that they name: `neighbours`: each row lists 128 different observations. The counts sum to 128; some device owns exactly 8; the exclusive prefix sum of counts at device d differs from d * 4 by at most 2.
All inputs are finite; a program needn't handle non-finite values.
Results may differ from a plain program's by a relative error of at most 0.0003.
Values sent between devices are 32-bit elements; how exact they have to be, the bound alone decides.
No kernel may reach another device: no remote copies, remote signals or barrier semaphores. Data moves between devices by JAX's collectives and lax.ppermute only.
A program may use at most 128 MiB of HBM per device.

v0:
```python
import jax
import jax.numpy as jnp
from jax import lax
from jax.sharding import PartitionSpec as P

S = 65536
LOC = 128
ZONE_GRIDPOINTS = 512
PREDICT_SUBTICKS = 24
MEM_DEV = 4
CAP = 8
LSCALE = 2048


FORCING = 8.0
TIME_STEP = 0.01
HIGH = lax.Precision.HIGHEST


def propagate_dynamics(lorenz_vector):
    tendency = (
        (jnp.roll(lorenz_vector, -1, axis=1) - jnp.roll(lorenz_vector, 2, axis=1))
        * jnp.roll(lorenz_vector, 1, axis=1)
        - lorenz_vector
        + FORCING
    )
    return lorenz_vector + TIME_STEP * tendency


def obs_error(zone_identifier, columns, obs_var, measured_indexes):
    centre = zone_identifier * ZONE_GRIDPOINTS + ZONE_GRIDPOINTS // 2
    gap_raw = jnp.abs(measured_indexes[columns] - centre)
    distance = jnp.minimum(gap_raw, S - gap_raw).astype(jnp.float32)
    scaled = distance / float(LSCALE)
    return obs_var[columns] * (1.0 + scaled * scaled)


def analyse(zone_gridpoint_matrix, obs_raw, innov_cols, errors):
    divisor = float(zone_gridpoint_matrix.shape[0] - 1)
    anomalies = zone_gridpoint_matrix - jnp.mean(zone_gridpoint_matrix, axis=0, keepdims=True)
    obs_anom = obs_raw - jnp.mean(obs_raw, axis=0, keepdims=True)
    obs_cov = jnp.dot(
        obs_anom.T, obs_anom, precision=HIGH, preferred_element_type=jnp.float32
    ) / divisor + jnp.diag(errors)
    factor = jnp.linalg.cholesky(obs_cov)
    solved = jax.scipy.linalg.cho_solve((factor, True), innov_cols.T)
    regression = (
        jnp.dot(obs_anom.T, anomalies, precision=HIGH, preferred_element_type=jnp.float32) / divisor
    )
    return zone_gridpoint_matrix + jnp.dot(
        solved.T, regression, precision=HIGH, preferred_element_type=jnp.float32
    )


def owner_slots(analysed, offsets, occupied, device_total):
    half_block = MEM_DEV // 2
    width = analysed.shape[1]
    front = jnp.zeros((half_block, width), jnp.float32)
    back = jnp.zeros((CAP + half_block, width), jnp.float32)
    padded_rows = jnp.concatenate([front, analysed, back], axis=0)
    parts_list = []
    for number in range((CAP + MEM_DEV) // MEM_DEV):
        begin = number * MEM_DEV
        parts_list.append(
            padded_rows[begin : begin + device_total * MEM_DEV].reshape(
                device_total, MEM_DEV, width
            )
        )
    windows = jnp.concatenate(parts_list, axis=1)
    relative = offsets - jnp.arange(device_total, dtype=jnp.int32) * MEM_DEV + half_block
    chosen_rows = jnp.zeros((device_total, CAP, width), jnp.float32)
    for start in range(MEM_DEV + 1):
        chosen_rows = jnp.where(
            (relative == start)[:, None, None], windows[:, start : start + CAP], chosen_rows
        )
    chosen_rows = jnp.where(occupied[:, :, None], chosen_rows, 0.0)
    return chosen_rows.reshape(device_total * CAP, width)


def per_device(
    prior_sample_matrix, obs_values, obs_var, measured_indexes, neighbours, perturbation, counts
):
    predict_trajectory = lax.fori_loop(
        0,
        PREDICT_SUBTICKS,
        lambda single_subtick, lorenz_vector: propagate_dynamics(lorenz_vector),
        prior_sample_matrix,
    )
    predicted_readings = predict_trajectory[:, measured_indexes]
    innovation = (
        obs_values[None, :] + jnp.sqrt(obs_var)[None, :] * perturbation - predicted_readings
    )
    accelerator_group = lax.axis_size(("member", "region"))
    gridpoint_total = predict_trajectory.shape[1] // accelerator_group
    reg_dev = gridpoint_total // ZONE_GRIDPOINTS
    device_index = lax.axis_index(("member", "region"))
    chosen = neighbours.reshape(-1)
    own_cells, chosen_equiv, chosen_innov = (
        lax.all_to_all(
            predict_trajectory, ("member", "region"), split_axis=1, concat_axis=0, tiled=True
        ),
        lax.all_to_all(
            predicted_readings[:, chosen],
            ("member", "region"),
            split_axis=1,
            concat_axis=0,
            tiled=True,
        ),
        lax.all_to_all(
            innovation[:, chosen], ("member", "region"), split_axis=1, concat_axis=0, tiled=True
        ),
    )
    pieces = []
    for number in range(reg_dev):
        zone_identifier = device_index * reg_dev + number
        columns = neighbours[zone_identifier]
        equiv_cols = chosen_equiv[:, number * LOC : (number + 1) * LOC]
        innov_cols = chosen_innov[:, number * LOC : (number + 1) * LOC]
        zone_gridpoint_matrix = own_cells[
            :, number * ZONE_GRIDPOINTS : (number + 1) * ZONE_GRIDPOINTS
        ]
        pieces.append(
            analyse(
                zone_gridpoint_matrix,
                equiv_cols,
                innov_cols,
                obs_error(zone_identifier, columns, obs_var, measured_indexes),
            )
        )
    analysed = jnp.concatenate(pieces, axis=1)
    offsets = jnp.cumsum(counts) - counts
    slot_index = jnp.arange(CAP, dtype=jnp.int32)
    occupied = slot_index[None, :] < counts[:, None]
    mine = occupied[device_index]
    outgoing = owner_slots(analysed, offsets, occupied, accelerator_group)
    owned = lax.all_to_all(outgoing, ("member", "region"), split_axis=0, concat_axis=1, tiled=True)
    owned = propagate_dynamics(owned)
    return jnp.where(mine[:, None], owned, 0.0)


def solution(mesh):
    in_specs = (
        P(("member", "region"), None),
        P(),
        P(),
        P(),
        P(),
        P(("member", "region"), None),
        P(),
    )
    out_specs = P(("member", "region"), None)
    return jax.shard_map(
        per_device, mesh=mesh, in_specs=in_specs, out_specs=out_specs, check_vma=False
    )
```

profile of v0, /device:TPU:1, one launch (start us, length us, event | category | flops | bytes accessed | tf_op | source)
XLA Modules:
  0.0 551.6 jit_solution(1071594539823870355)
XLA Ops:
  2.3 197.9 %while.10 = (s32[]{:T(128)}, f32[4,65536]{1,0:T(4,128)}, s32[]{:T(128)}) while((s32[]{:T(128)}, f32[4,65536]{1,0:T(4,128)}, s32[]{:T(128)}) %tuple.49), condition=%wide.region_2.3_spmd, body=%wide.region_1.2_spmd.sunk | while | flops 2359298 | bytes 11534381 | solution.py:83
  56.7 3.3 fusion.113
  73.2 3.3 fusion.113
  89.7 3.3 fusion.113
  106.1 3.3 fusion.113
  200.2 16.4 %copy.40 = f32[4,65536]{0,1:T(8,128)} copy(f32[4,65536]{1,0:T(4,128)} %get-tuple-element.19) | data formatting | bytes 2097152 | tf_op jit(solution)/shard_map/while | solution.py:83
  216.6 13.4 %gather_fusion = f32[1024,4]{1,0:T(8,128)S(1)} fusion(f32[4,65536]{0,1:T(8,128)} %copy.40, s32[1024]{0:T(1024)S(1)} %fusion.63), kind=kCustom, calls=%fused_computation | custom fusion | bytes 36864 | tf_op jit(solution)/shard_map/gather | solution.py:89
  230.5 54.4 %gather_fusion.4 = f32[16384,4]{1,0:T(8,128)} fusion(f32[4,1024]{0,1:T(8,128)S(1)} %copy.46, s32[16384]{0:T(1024)S(1)} %broadcast_clamp_fusion), kind=kCustom, calls=%fused_computation.4 | custom fusion | bytes 589824 | tf_op jit(solution)/shard_map/gather | solution.py:110
  285.0 5.9 %copy.47 = f32[4,32,512]{2,0,1:T(4,128)} copy(f32[4,32,512]{0,2,1:T(8,128)} %bitcast.130) | data formatting | bytes 524288 | tf_op jit(solution)/shard_map/all_to_all | solution.py:109
  290.9 7.1 %all-to-all-start.2 = ((f32[4,32,512]{2,0,1:T(4,128)}), f32[4,32,512]{2,0,1:T(4,128)S(1)}, u32[]{:S(2)}, u32[]{:S(2)}) async-start(f32[4,32,512]{2,0,1:T(4,128)} %copy.47), calls=%async_computation.2 | async-start | bytes 524288 | tf_op jit(solution)/shard_map/all_to_all | solution.py:109
  306.1 54.4 %gather_fusion.1 = f32[16384,4]{1,0:T(8,128)} fusion(f32[4,1024]{0,1:T(8,128)S(1)} %copy.42, s32[16384]{0:T(1024)S(1)} %broadcast_clamp_fusion), kind=kCustom, calls=%fused_computation.1 | custom fusion | bytes 589824 | tf_op jit(solution)/shard_map/gather | solution.py:103
  360.6 5.9 %copy.43 = f32[4,32,512]{2,0,1:T(4,128)} copy(f32[4,32,512]{0,2,1:T(8,128)} %bitcast.129) | data formatting | bytes 524288 | tf_op jit(solution)/shard_map/all_to_all | solution.py:102
  366.8 5.8 %all-to-all-start.1 = ((f32[4,32,512]{2,0,1:T(4,128)}), f32[4,32,512]{2,0,1:T(4,128)S(1)}, u32[]{:S(2)}, u32[]{:S(2)}) async-start(f32[4,32,512]{2,0,1:T(4,128)} %copy.43), calls=%async_computation.1 | async-start | bytes 524288 | tf_op jit(solution)/shard_map/all_to_all | solution.py:102
  372.8 10.1 %all-to-all-done.1 = f32[4,32,512]{2,0,1:T(4,128)S(1)} async-done(((f32[4,32,512]{2,0,1:T(4,128)}), f32[4,32,512]{2,0,1:T(4,128)S(1)}, u32[]{:S(2)}, u32[]{:S(2)}) %all-to-all-start.1) | async-done | bytes 262176 | tf_op jit(solution)/shard_map/all_to_all | solution.py:102
  386.3 11.7 %cholesky.107 = f32[128,128]{1,0:T(8,128)S(1)} custom-call(f32[128,128]{1,0:T(8,128)S(1)} %fusion.42), custom_call_target="Cholesky" | custom-call | tf_op jit(solution)/shard_map/jit(cholesky)/cholesky | solution.py:45
  399.4 9.8 %custom-call.13 = f32[1,128,128]{1,2,0:T(8,128)S(1)} custom-call(f32[1,128,128]{2,1,0:T(8,128)S(1)} %fusion.34), custom_call_target="InvertDiagBlocksLowerTriangular" | custom-call | tf_op jit(solution)/shard_map/jit(_cho_solve)/triangular_solve | solution.py:46
  409.7 11.7 %cholesky.96 = f32[128,128]{1,0:T(8,128)S(1)} custom-call(f32[128,128]{1,0:T(8,128)S(1)} %fusion.46), custom_call_target="Cholesky" | custom-call | tf_op jit(solution)/shard_map/jit(cholesky)/cholesky | solution.py:45
  422.9 10.0 %custom-call.12 = f32[1,128,128]{1,2,0:T(8,128)S(1)} custom-call(f32[1,128,128]{2,1,0:T(8,128)S(1)} %fusion.33), custom_call_target="InvertDiagBlocksLowerTriangular" | custom-call | tf_op jit(solution)/shard_map/jit(_cho_solve)/triangular_solve | solution.py:46
  433.3 11.7 %cholesky.85 = f32[128,128]{1,0:T(8,128)S(1)} custom-call(f32[128,128]{1,0:T(8,128)S(1)} %fusion.50), custom_call_target="Cholesky" | custom-call | tf_op jit(solution)/shard_map/jit(cholesky)/cholesky | solution.py:45
  446.5 9.8 %custom-call.11 = f32[1,128,128]{1,2,0:T(8,128)S(1)} custom-call(f32[1,128,128]{2,1,0:T(8,128)S(1)} %fusion.32), custom_call_target="InvertDiagBlocksLowerTriangular" | custom-call | tf_op jit(solution)/shard_map/jit(_cho_solve)/triangular_solve | solution.py:46
  456.7 11.7 %cholesky.74 = f32[128,128]{1,0:T(8,128)S(1)} custom-call(f32[128,128]{1,0:T(8,128)S(1)} %fusion.54), custom_call_target="Cholesky" | custom-call | tf_op jit(solution)/shard_map/jit(cholesky)/cholesky | solution.py:45
  469.9 10.0 %custom-call.10 = f32[1,128,128]{1,2,0:T(8,128)S(1)} custom-call(f32[1,128,128]{2,1,0:T(8,128)S(1)} %fusion.31), custom_call_target="InvertDiagBlocksLowerTriangular" | custom-call | tf_op jit(solution)/shard_map/jit(_cho_solve)/triangular_solve | solution.py:46
  493.5 5.9 %all-to-all-start.3 = ((f32[32,8,2048]{2,1,0:T(8,128)}), f32[32,8,2048]{2,1,0:T(8,128)S(1)}, u32[]{:S(2)}, u32[]{:S(2)}) async-start(f32[32,8,2048]{2,1,0:T(8,128)} %fusion.8), calls=%async_computation.3 | async-start | bytes 4194304 | tf_op jit(solution)/shard_map/all_to_all | solution.py:136
  499.3 48.3 %all-to-all-done.3 = f32[32,8,2048]{2,1,0:T(8,128)S(1)} async-done(((f32[32,8,2048]{2,1,0:T(8,128)}), f32[32,8,2048]{2,1,0:T(8,128)S(1)}, u32[]{:S(2)}, u32[]{:S(2)}) %all-to-all-start.3) | async-done | bytes 2097184 | tf_op jit(solution)/shard_map/all_to_all | solution.py:136
  (222 shorter events, 223.0 us)
Async XLA Ops:
  0.0 2.3 copy-start
  200.2 16.4 %copy-start.1 = (s32[1024]{0:T(1024)S(1)}, s32[1024]{0:T(1024)}, u32[]{:S(2)}) copy-start(s32[1024]{0:T(1024)} %param.15) | copy-start | bytes 12292
  200.2 30.0 %copy-start.3 = (f32[4,1024]{1,0:T(4,128)S(1)}, f32[4,1024]{1,0:T(4,128)}, u32[]{:S(2)}) copy-start(f32[4,1024]{1,0:T(4,128)} %param.17) | copy-start | bytes 49156
  200.2 30.0 %copy-start.5 = (f32[1024]{0:T(1024)S(1)}, f32[1024]{0:T(1024)}, u32[]{:S(2)}) copy-start(f32[1024]{0:T(1024)} %param.13) | copy-start | bytes 12292
  200.2 30.2 %copy-start.2 = (s32[128,128]{1,0:T(8,128)S(1)}, s32[128,128]{1,0:T(8,128)}, u32[]{:S(2)}) copy-start(s32[128,128]{1,0:T(8,128)} %param.16) | copy-start | bytes 196612
  290.9 75.9 %all-to-all-start.2 = ((f32[4,32,512]{2,0,1:T(4,128)}), f32[4,32,512]{2,0,1:T(4,128)S(1)}, u32[]{:S(2)}, u32[]{:S(2)}) async-start(f32[4,32,512]{2,0,1:T(4,128)} %copy.47), calls=%async_computation.2 | async-start | bytes 524288 | tf_op jit(solution)/shard_map/all_to_all | solution.py:109
  360.6 5.9 %copy-start.4 = (s32[32]{0:T(128)S(1)}, s32[32]{0:T(128)}, u32[]{:S(2)}) copy-start(s32[32]{0:T(128)} %param.18) | copy-start | bytes 388
  366.8 16.2 %all-to-all-start.1 = ((f32[4,32,512]{2,0,1:T(4,128)}), f32[4,32,512]{2,0,1:T(4,128)S(1)}, u32[]{:S(2)}, u32[]{:S(2)}) async-start(f32[4,32,512]{2,0,1:T(4,128)} %copy.43), calls=%async_computation.1 | async-start | bytes 524288 | tf_op jit(solution)/shard_map/all_to_all | solution.py:102
  382.9 99.0 %all-to-all-start = ((f32[4,32,2048]{2,0,1:T(4,128)}), f32[4,32,2048]{2,0,1:T(4,128)S(1)}, u32[]{:S(2)}, u32[]{:S(2)}) async-start(f32[4,32,2048]{2,0,1:T(4,128)} %bitcast.2), calls=%async_computation | async-start | bytes 2097152 | tf_op jit(solution)/shard_map/all_to_all | solution.py:99
  493.5 54.2 %all-to-all-start.3 = ((f32[32,8,2048]{2,1,0:T(8,128)}), f32[32,8,2048]{2,1,0:T(8,128)S(1)}, u32[]{:S(2)}, u32[]{:S(2)}) async-start(f32[32,8,2048]{2,1,0:T(8,128)} %fusion.8), calls=%async_computation.3 | async-start | bytes 4194304 | tf_op jit(solution)/shard_map/all_to_all | solution.py:136
where the time goes:
time: 561 us; the launch traced here: 552 us
  local copies, waits for them, and re-layouts  284 us (51%)
  other arithmetic  180 us (32%)
  waiting for transfers between devices  58.4 us (10%)
  starting transfers between devices  21.5 us (4%)
  matrix products  6.48 us (1%)
    add x24, other arithmetic, propagate_dynamics(): return lorenz_vector + TIME_STEP * tendency  80.4 us
    slice x50, local copies, waits for them, and re-layouts, propagate_dynamics(): jnp.roll(lorenz_vector, 1, axis=1)  70.6 us
    gather x1, local copies, waits for them, and re-layouts, per_device(): innovation[:, chosen]  54.4 us
    gather x1, local copies, waits for them, and re-layouts, per_device(): predicted_readings[:, chosen]  54.4 us
    another operation x12, other arithmetic, analyse(): factor = jnp.linalg.cholesky(obs_cov)  49.9 us
    all_to_all x1, waiting for transfers between devices, per_device(): lax.all_to_all(outgoing, ('member', 'region'), split_axis=0, concat_axis=...  48.3 us
    another operation x8, other arithmetic, analyse(): solved = jax.scipy.linalg.cho_solve((factor, True), innov_cols.T)  42.4 us
    while x24, local copies, waits for them, and re-layouts  29.5 us
  transfers between devices with their start and end apart: 4, of which 2 were waited for; matrix products, arithmetic and copies ran while one was open for 30% of the time, Pallas kernels for 0%

commit v1 on v0

v1 whole, which is shorter than its diff:
```python
import functools

import jax
import jax.numpy as jnp
from jax import lax
from jax.experimental import pallas as pl
from jax.experimental.pallas import tpu as pltpu
from jax.sharding import PartitionSpec as P

PREDICT_SUBTICKS = 24
CAP = 8
LSCALE = 2048
FORCING = 8.0
TIME_STEP = 0.01
HIGH = lax.Precision.HIGHEST
AXES = ("member", "region")
LANES = 128
ROWS = 8


def lanes_iota():
    return lax.broadcasted_iota(jnp.int32, (ROWS, LANES), 1)


def rows_iota():
    return lax.broadcasted_iota(jnp.int32, (ROWS, LANES), 0)


def forecast_kernel(slot_ref, turn_ref, part_ref, x_ref, state_ref, readings_ref, *, devices, members):
    parts = ROWS // members
    steps = state_ref.shape[0] // devices // ROWS
    total = devices * steps
    lane = lanes_iota()
    row = rows_iota()
    first_lane = lane == 0
    low_lanes = lane < 2
    last_lane = lane == LANES - 1
    first_part = row < members
    last_part = row >= ROWS - members

    for destination in range(devices):
        for part in range(parts):
            for step in range(steps):
                tile = (destination * parts + part) * steps + step
                begin = (destination * steps + step) * ROWS + part * members
                state_ref[begin : begin + members, :] = x_ref[:, tile * LANES : (tile + 1) * LANES] * TIME_STEP

    def load(number):
        return state_ref[number * ROWS : (number + 1) * ROWS, :]

    def substep(_, carry):
        wrap_first = pltpu.roll(load(0), ROWS - members, axis=0)
        below = pltpu.roll(load(total - 1), members, axis=0)
        for destination in range(devices):
            start = destination * steps
            own_last = pltpu.roll(load(start + steps - 1), members, axis=0)
            previous = jnp.where(first_part, below, own_last)
            below = own_last
            if destination == 0:
                own_first = wrap_first
            else:
                own_first = next_first
            if destination + 1 < devices:
                next_first = pltpu.roll(load(start + steps), ROWS - members, axis=0)
            else:
                next_first = wrap_first
            following = jnp.where(last_part, next_first, own_first)
            previous_one = pltpu.roll(previous, 1, axis=1)
            previous_two = pltpu.roll(previous, 2, axis=1)
            current = load(start)
            current_up = pltpu.roll(current, LANES - 1, axis=1)
            for step in range(steps):
                after = load(start + step + 1) if step + 1 < steps else following
                after_up = pltpu.roll(after, LANES - 1, axis=1)
                one = pltpu.roll(current, 1, axis=1)
                two = pltpu.roll(current, 2, axis=1)
                left = jnp.where(first_lane, previous_one, one)
                left_two = jnp.where(low_lanes, previous_two, two)
                right = jnp.where(last_lane, after_up, current_up)
                updated = (current * (1.0 - TIME_STEP) + FORCING * TIME_STEP * TIME_STEP) + (right - left_two) * left
                begin = (start + step) * ROWS
                state_ref[begin : begin + ROWS, :] = updated
                previous_one, previous_two = one, two
                current, current_up = after, after_up
        return carry

    lax.fori_loop(0, PREDICT_SUBTICKS, substep, 0)

    for number in range(total):
        begin = number * ROWS
        state_ref[begin : begin + ROWS, :] = load(number) * (1.0 / TIME_STEP)

    def gather(block, carry):
        base = block * LANES
        picked = [jnp.zeros((ROWS, LANES), jnp.float32) for _ in range(4)]
        for number in range(LANES):
            begin = pl.multiple_of(slot_ref[base + number] * ROWS, ROWS)
            turned = pltpu.roll(state_ref[pl.ds(begin, ROWS), :], turn_ref[base + number], axis=1)
            picked[number % 4] = jnp.where(lane == number, turned, picked[number % 4])
        both = picked[0]
        for number in range(1, 4):
            both = jnp.where(lane % 4 == number, picked[number], both)
        part_of = part_ref[pl.ds(block, 1), :]
        chosen = both
        for part in range(1, parts):
            chosen = jnp.where(part_of == part, pltpu.roll(both, ROWS - part * members, axis=0), chosen)
        for destination in range(devices):
            readings_ref[destination, pl.ds(block * members, members), :] = chosen[:members]
        return carry

    lax.fori_loop(0, part_ref.shape[0], gather, 0)


def dot(a, b, contract, precision=HIGH):
    return lax.dot_general(a, b, (contract, ((), ())), precision=precision, preferred_element_type=jnp.float32)


def invert_all(matrix_ref):
    regions, size, _ = matrix_ref.shape
    lane = lanes_iota()
    row = rows_iota()

    def column(value, index):
        return jnp.take_along_axis(value, jnp.full((ROWS, LANES), index, jnp.int32), axis=1)

    def panel(number, carry):
        base = number * ROWS
        start = pl.multiple_of(base, ROWS)
        inside = (lane >= base) & (lane < base + ROWS)
        unit = jnp.where(lane - base == row, 1.0, 0.0)
        finished = []
        for region in range(regions):
            block = matrix_ref[region, pl.ds(start, ROWS), :]
            columns = [column(block, base + k) for k in range(ROWS)]
            block = jnp.where(inside, unit, block)
            for j in range(ROWS):
                inverse = 1.0 / columns[j][j : j + 1, :]
                here = row == j
                scaled = block[j : j + 1, :] * inverse
                block = jnp.where(here, scaled, block - columns[j] * scaled)
                for k in range(j + 1, ROWS):
                    scaled = columns[k][j : j + 1, :] * inverse
                    columns[k] = jnp.where(here, scaled, columns[k] - columns[j] * scaled)
            finished.append(block)
        for region in range(regions):
            block = finished[region]
            for i in range(size // ROWS):
                other = matrix_ref[region, i * ROWS : (i + 1) * ROWS, :]
                result = jnp.where(inside, 0.0, other)
                for k in range(ROWS):
                    result = result - column(other, base + k) * block[k : k + 1, :]
                matrix_ref[region, i * ROWS : (i + 1) * ROWS, :] = result
            matrix_ref[region, pl.ds(start, ROWS), :] = block
        return carry

    lax.fori_loop(0, size // ROWS, panel, 0)


def solve_kernel(
    zone_ref, neighbours_ref, table_ref, readings_ref, noise_ref, transform_ref, stack_ref, pieces_ref, matrix_ref, *, cells, zone_cells
):
    devices, _, _ = readings_ref.shape
    regions, total, _ = transform_ref.shape
    members = total // devices
    observations = table_ref.shape[1]
    extra = stack_ref.shape[0] - 2 * total
    for block in range(observations // LANES):
        lanes = slice(block * LANES, (block + 1) * LANES)
        values = table_ref[0:1, lanes]
        spread = jnp.sqrt(table_ref[1:2, lanes])
        for source in range(devices):
            equivalents = readings_ref[source, block * members : (block + 1) * members, :]
            noise = noise_ref[source, block * members : (block + 1) * members, :]
            stack_ref[source * members : (source + 1) * members, lanes] = equivalents
            stack_ref[total + source * members : total + (source + 1) * members, lanes] = values + spread * noise - equivalents
    stack_ref[2 * total : 2 * total + ROWS, :] = table_ref[...]
    stack_ref[2 * total + ROWS :, :] = jnp.zeros((extra - ROWS, observations), jnp.float32)
    height = stack_ref.shape[0]
    rest = stack_ref[...]
    for piece in range(3):
        rounded = rest.astype(jnp.bfloat16)
        pieces_ref[piece * height : (piece + 1) * height, :] = rounded
        rest = rest - rounded.astype(jnp.float32)

    centre0 = zone_ref[0] * zone_cells + zone_cells // 2
    size = neighbours_ref.shape[1]
    diagonal = lax.broadcasted_iota(jnp.int32, (size, size), 0) == lax.broadcasted_iota(jnp.int32, (size, size), 1)
    ids = lax.broadcasted_iota(jnp.int32, (observations, size), 0)
    anomalies, innovations = [], []
    for region in range(regions):
        pick = jnp.where(ids == neighbours_ref[region : region + 1, :], 1.0, 0.0).astype(jnp.bfloat16)
        picked = dot(pieces_ref[...], pick, ((1,), (0,)), lax.Precision.DEFAULT)
        picked = picked[:height] + picked[height : 2 * height] + picked[2 * height :]
        equivalents = picked[:total]
        innovations.append(picked[total : 2 * total])
        variance = picked[2 * total + 1 : 2 * total + 2]
        place = picked[2 * total + 2 : 2 * total + 3]
        centre = (centre0 + region * zone_cells).astype(jnp.float32)
        gap = jnp.abs(place - centre)
        scaled = jnp.minimum(gap, cells - gap) / float(LSCALE)
        errors = variance * (1.0 + scaled * scaled)
        anomaly = equivalents - jnp.sum(equivalents, axis=0, keepdims=True) * (1.0 / total)
        anomalies.append(anomaly)
        covariance = dot(anomaly, anomaly, ((0,), (0,))) * (1.0 / (total - 1))
        matrix_ref[region, :, :] = jnp.where(diagonal, covariance + errors, covariance)
    invert_all(matrix_ref)
    for region in range(regions):
        weights = dot(innovations[region], matrix_ref[region], ((1,), (0,)))
        transform_ref[region, :, :] = dot(weights, anomalies[region], ((1,), (1,))) * (1.0 / (total - 1))


def apply_kernel(counts_ref, transform_ref, cells_ref, owned_ref, block_ref, result_ref):
    sources, height, _ = cells_ref.shape
    regions, total, _ = transform_ref.shape
    members = total // sources
    parts = ROWS // members
    steps = height // ROWS
    tiles = parts * steps
    wide = tiles // regions
    for part in range(parts):
        for step in range(steps):
            tile = part * steps + step
            region, place = tile // wide, tile % wide
            begin = step * ROWS + part * members
            for source in range(sources):
                block_ref[region, source * members : (source + 1) * members, place * LANES : (place + 1) * LANES] = cells_ref[
                    source, begin : begin + members, :
                ]
    for region in range(regions):
        block = block_ref[region]
        anomalies = block - jnp.sum(block, axis=0, keepdims=True) * (1.0 / total)
        analysed = block + dot(transform_ref[region], anomalies, ((1,), (0,)))
        for place in range(wide):
            result_ref[region * wide + place, :total, :] = analysed[:, place * LANES : (place + 1) * LANES]
    for tile in range(tiles):
        result_ref[tile, total:, :] = jnp.zeros((ROWS, LANES), jnp.float32)

    def window(destination, offset):
        for tile in range(tiles):
            owned_ref[destination, tile * ROWS : (tile + 1) * ROWS, :] = result_ref[tile, pl.ds(offset, CAP), :]
        return offset + counts_ref[destination]

    lax.fori_loop(0, sources, window, jnp.int32(0))


def advance_kernel(count_ref, rows_ref, out_ref):
    tiles = rows_ref.shape[0] // ROWS
    here = out_ref.shape[1] // LANES
    lane = lanes_iota()
    occupied = rows_iota() < count_ref[0]
    start = pl.program_id(0) * here

    def load(number):
        return rows_ref[pl.ds(pl.multiple_of(number * ROWS, ROWS), ROWS), :]

    before = load(lax.rem(start + tiles - 1, tiles))
    before_one = pltpu.roll(before, 1, axis=1)
    before_two = pltpu.roll(before, 2, axis=1)
    current = load(start)
    current_up = pltpu.roll(current, LANES - 1, axis=1)
    for tile in range(here):
        after = load(start + tile + 1) if tile + 1 < here else load(lax.rem(start + here, tiles))
        after_up = pltpu.roll(after, LANES - 1, axis=1)
        one = pltpu.roll(current, 1, axis=1)
        two = pltpu.roll(current, 2, axis=1)
        left = jnp.where(lane == 0, before_one, one)
        left_two = jnp.where(lane < 2, before_two, two)
        right = jnp.where(lane == LANES - 1, after_up, current_up)
        stepped = current + TIME_STEP * ((right - left_two) * left - current + FORCING)
        out_ref[:, tile * LANES : (tile + 1) * LANES] = jnp.where(occupied, stepped, 0.0)
        before_one, before_two = one, two
        current, current_up = after, after_up


def whole(space=pltpu.VMEM):
    return pl.BlockSpec(memory_space=space)


def per_device(prior_sample_matrix, obs_values, obs_var, measured_indexes, neighbours, perturbation, counts):
    devices = lax.axis_size(AXES)
    device_index = lax.axis_index(AXES)
    members, cells = prior_sample_matrix.shape
    total = members * devices
    observations = obs_values.shape[0]
    zones, local = neighbours.shape
    regions = zones // devices
    zone_cells = cells // zones
    parts = ROWS // members
    share = cells // devices
    steps = share // LANES // parts
    blocks = observations // LANES

    slot = (measured_indexes // share) * steps + (measured_indexes // LANES) % steps
    part = (measured_indexes // (LANES * steps)) % parts
    turn = (jnp.arange(observations, dtype=jnp.int32) - measured_indexes) % LANES
    state, readings = pl.pallas_call(
        functools.partial(forecast_kernel, devices=devices, members=members),
        out_shape=(
            jax.ShapeDtypeStruct((devices * steps * ROWS, LANES), jnp.float32),
            jax.ShapeDtypeStruct((devices, blocks * members, LANES), jnp.float32),
        ),
        in_specs=[whole(pltpu.SMEM), whole(pltpu.SMEM), whole(), whole()],
        out_specs=(whole(), whole()),
        name="forecast",
    )(slot, turn, part.reshape(blocks, LANES), prior_sample_matrix)

    noise = perturbation.reshape(members, blocks, LANES).transpose(1, 0, 2).reshape(1, blocks * members, LANES)
    exchange = functools.partial(lax.all_to_all, axis_name=AXES, split_axis=0, concat_axis=0, tiled=True)
    noise = exchange(jnp.broadcast_to(noise, (devices, blocks * members, LANES)))
    readings = exchange(readings)
    own_cells = exchange(state.reshape(devices, steps * ROWS, LANES))

    zone = device_index * regions
    table = jnp.stack([obs_values, obs_var, measured_indexes.astype(jnp.float32)])
    table = jnp.concatenate([table, jnp.zeros((ROWS - 3, observations), jnp.float32)])
    height = 2 * total + 2 * ROWS
    transform = pl.pallas_call(
        functools.partial(solve_kernel, cells=float(cells), zone_cells=zone_cells),
        out_shape=jax.ShapeDtypeStruct((regions, total, total), jnp.float32),
        in_specs=[whole(pltpu.SMEM), whole(), whole(), whole(), whole()],
        out_specs=whole(),
        scratch_shapes=[
            pltpu.VMEM((height, observations), jnp.float32),
            pltpu.VMEM((3 * height, observations), jnp.bfloat16),
            pltpu.VMEM((regions, local, local), jnp.float32),
        ],
        name="solve",
    )(zone.reshape(1), lax.dynamic_slice_in_dim(neighbours, zone, regions, 0), table, readings, noise)

    tiles = share // LANES
    outgoing = pl.pallas_call(
        apply_kernel,
        out_shape=jax.ShapeDtypeStruct((devices, tiles * CAP, LANES), jnp.float32),
        in_specs=[whole(pltpu.SMEM), whole(), whole()],
        out_specs=whole(),
        scratch_shapes=[
            pltpu.VMEM((regions, total, zone_cells), jnp.float32),
            pltpu.VMEM((tiles, total + ROWS, LANES), jnp.float32),
        ],
        name="analyse",
    )(counts, transform, own_cells)
    owned = exchange(outgoing).reshape(devices * tiles * CAP, LANES)

    chunks = 8
    return pl.pallas_call(
        advance_kernel,
        grid=(chunks,),
        out_shape=jax.ShapeDtypeStruct((CAP, cells), jnp.float32),
        in_specs=[whole(pltpu.SMEM), whole()],
        out_specs=pl.BlockSpec((CAP, cells // chunks), lambda i: (0, i)),
        name="advance",
    )(lax.dynamic_slice_in_dim(counts, device_index, 1, 0), owned)


def solution(mesh):
    rows = P(AXES, None)
    return jax.shard_map(
        per_device, mesh=mesh, in_specs=(rows, P(), P(), P(), P(), rows, P()), out_specs=rows, check_vma=False
    )
```

time: 561 us -> 168 us (0.30); the launches traced: 552 us -> 168 us
  local copies, waits for them, and re-layouts: 284 us -> 5.24 us
  other arithmetic: 180 us -> 2.05 us
  Pallas kernels: 0 us -> 75.2 us
  blocking collectives: 0 us -> 21.2 us
  waiting for transfers between devices: 58.4 us -> 47.7 us
  matrix products: 6.48 us -> 0 us
    gather x13 -> x0, local copies, waits for them, and re-layouts: 130 us -> none  [the longest x1 54.4 us: per_device(): innovation[:, chosen]]
    another operation x22 -> x0, other arithmetic: 92.5 us -> none  [the longest x12 49.9 us: analyse(): factor = jnp.linalg.cholesky(obs_cov)]
    slice x76 -> x0, local copies, waits for them, and re-layouts: 90.1 us -> none  [the longest x50 70.6 us: propagate_dynamics(): jnp.roll(lorenz_vector, 1, axis=1)]
    add x24 -> x0, other arithmetic: 80.4 us -> none  [propagate_dynamics(): return lorenz_vector + TIME_STEP * tendency]
    pallas_call x0 -> x4, Pallas kernels: none -> 75.2 us  [the longest x1 36.1 us: per_device(): pl.pallas_call(functools.partial(solve_kernel, cells=float(cells), zone_c...]
    while x25 -> x0, local copies, waits for them, and re-layouts: 45.9 us -> none
    all_to_all x0 -> x1, blocking collectives: none -> 21.2 us  [per_device(): readings = exchange(readings)]
    all_to_all x5 -> x0, local copies, waits for them, and re-layouts: 12.4 us -> none  [the longest x2 6 us: per_device(): lax.all_to_all(predicted_readings[:, chosen], ('member', 'region'), split...]
  transfers between devices with their start and end apart: 4 -> 3, of which waited for: 2 -> 1; matrix products, arithmetic and copies ran while one was open for 30% -> 2% of each run, Pallas kernels for 0% -> 39%
where the time goes in v1:
time: 168 us
  Pallas kernels  75.2 us (45%)
  waiting for transfers between devices  47.7 us (28%)
  blocking collectives  21.2 us (13%)
  starting transfers between devices  16.1 us (10%)
  local copies, waits for them, and re-layouts  5.24 us (3%)
  other arithmetic  2.05 us (1%)
    all_to_all x1, waiting for transfers between devices, per_device(): owned = exchange(outgoing).reshape(devices * tiles * CAP, LANES)  47.7 us
    pallas_call x1, Pallas kernels, per_device(): pl.pallas_call(functools.partial(solve_kernel, cells=float(cells), zone_c...  36.1 us
    pallas_call x1, Pallas kernels, per_device(): pl.pallas_call(functools.partial(forecast_kernel, devices=devices, member...  28.6 us
    all_to_all x1, blocking collectives, per_device(): readings = exchange(readings)  21.2 us
    all_to_all x1, starting transfers between devices, per_device(): exchange(jnp.broadcast_to(noise, (devices, blocks * members, LANES)))  7.08 us
    pallas_call x1, Pallas kernels, per_device(): pl.pallas_call(advance_kernel, grid=(chunks,), out_shape=jax.ShapeDtypeSt...  6.45 us
    all_to_all x1, starting transfers between devices, per_device(): owned = exchange(outgoing).reshape(devices * tiles * CAP, LANES)  5.83 us
    pallas_call x1, Pallas kernels, per_device(): pl.pallas_call(apply_kernel, out_shape=jax.ShapeDtypeStruct((devices, til...  4.1 us
  transfers between devices with their start and end apart: 3, of which 1 were waited for; matrix products, arithmetic and copies ran while one was open for 2% of the time, Pallas kernels for 39%

profile of v1, /device:TPU:1, one launch (start us, length us, event | category | flops | bytes accessed | tf_op | source)
XLA Modules:
  0.0 167.5 jit_solution(4192141865581974899)
XLA Ops:
  0.0 0.0 copy-start
  0.0 0.8 copy.11
  0.8 0.9 broadcast_in_dim.12
  1.6 7.1 %all-to-all-start.1 = ((f32[32,32,128]{2,1,0:T(8,128)}), f32[32,32,128]{2,1,0:T(8,128)S(1)}, u32[]{:S(2)}, u32[]{:S(2)}) async-start(f32[32,32,128]{2,1,0:T(8,128)} %broadcast_in_dim.12), calls=%async_computation.1 | async-start | bytes 1048576 | tf_op jit(solution)/shard_map/all_to_all | solution.py:309
  8.7 1.4 fusion.8
  10.1 28.6 %forecast.1 = (f32[2048,128]{1,0:T(8,128)}, f32[32,32,128]{2,1,0:T(8,128)}) custom-call(s32[1024]{0:T(1024)} %get-tuple-element.10.slot_ref, s32[1024]{0:T(1024)} %get-tuple-element.12.turn_ref, s32[8,128]{1,0:T(8,128)} %get-tuple-element.9.part_ref, f32[4,65536]{1,0:T(4,128)} %x_ref.1), custom_call_target="tpu_custom_call" | custom-call | tf_op jit(solution)/shard_map/forecast/pallas_call | solution.py:296
  38.6 0.0 all-to-all-done.1.noise_ref
  38.7 21.2 %all_to_all.20.readings_ref = f32[32,32,128]{2,1,0:T(8,128)} all-to-all(f32[32,32,128]{2,1,0:T(8,128)} %get-tuple-element.7), channel_id=1, replica_groups=mesh['member'=8,'region'=4] {'member','region'}, dimensions={0} | all-to-all | bytes 1048576 | tf_op jit(solution)/shard_map/all_to_all | solution.py:310
  59.9 3.2 %all-to-all-start.2 = ((f32[32,64,128]{2,1,0:T(8,128)}), f32[32,64,128]{2,1,0:T(8,128)S(1)}, u32[]{:S(2)}, u32[]{:S(2)}) async-start(f32[32,64,128]{2,1,0:T(8,128)} %bitcast.17), calls=%async_computation.2 | async-start | bytes 2097152 | tf_op jit(solution)/shard_map/all_to_all | solution.py:311
  63.0 0.1 pad.3.clone
  63.1 0.0 copy-done
  63.1 0.6 constant_dynamic-slice_fusion.neighbours_ref
  63.7 0.0 copy-done.4
  63.7 0.0 copy-done.5
  63.7 0.7 maximum_maximum_fusion.table_ref
  64.4 36.1 %solve.1.transform_ref = f32[4,128,128]{2,1,0:T(8,128)} custom-call(s32[1]{0:T(128)} %bitcast.zone_ref, s32[4,128]{1,0:T(4,128)} %constant_dynamic-slice_fusion.neighbours_ref, f32[8,1024]{1,0:T(8,128)} %maximum_maximum_fusion.table_ref, f32[32,32,128]{2,1,0:T(8,128)} %all_to_all.20.readings_ref, f32[32,32,128]{2,1,0:T(8,128)} %copy-done.3), custom_call_target="tpu_custom_call" | custom-call | tf_op jit(solution)/shard_map/solve/pallas_call | solution.py:317
  100.5 0.0 all-to-all-done.2.cells_ref
  100.5 1.0 copy-done.2
  101.5 4.1 %analyse.1 = f32[32,128,128]{2,1,0:T(8,128)} custom-call(s32[32]{0:T(128)} %counts_ref.1, f32[4,128,128]{2,1,0:T(8,128)} %solve.1.transform_ref, f32[32,64,128]{2,1,0:T(8,128)} %copy-done.2), custom_call_target="tpu_custom_call" | custom-call | tf_op jit(solution)/shard_map/analyse/pallas_call | solution.py:331
  105.6 5.8 %all-to-all-start.3 = ((f32[32,128,128]{2,1,0:T(8,128)}), f32[32,128,128]{2,1,0:T(8,128)S(1)}, u32[]{:S(2)}, u32[]{:S(2)}) async-start(f32[32,128,128]{2,1,0:T(8,128)} %analyse.1), calls=%async_computation.3 | async-start | bytes 4194304 | tf_op jit(solution)/shard_map/all_to_all | solution.py:342
  111.4 0.6 dynamic_slice.6.count_ref
  112.0 47.7 %all-to-all-done.3 = f32[32,128,128]{2,1,0:T(8,128)S(1)} async-done(((f32[32,128,128]{2,1,0:T(8,128)}), f32[32,128,128]{2,1,0:T(8,128)S(1)}, u32[]{:S(2)}, u32[]{:S(2)}) %all-to-all-start.3) | async-done | bytes 2097184 | tf_op jit(solution)/shard_map/all_to_all | solution.py:342
  159.7 1.3 copy-done.1
  161.1 6.4 %advance.1 = f32[8,65536]{1,0:T(8,128)} custom-call(s32[1]{0:T(128)} %dynamic_slice.6.count_ref, f32[4096,128]{1,0:T(8,128)} %bitcast.16), custom_call_target="tpu_custom_call" | custom-call | tf_op jit(solution)/shard_map/advance/pallas_call | solution.py:345
  (10 shorter events, 0.0 us)
Async XLA Ops:
  0.0 63.1 %copy-start = (s32[128,128]{1,0:T(8,128)S(1)}, s32[128,128]{1,0:T(8,128)}, u32[]{:S(2)}) copy-start(s32[128,128]{1,0:T(8,128)} %param.11) | copy-start | bytes 196612
  1.6 37.0 %all-to-all-start.1 = ((f32[32,32,128]{2,1,0:T(8,128)}), f32[32,32,128]{2,1,0:T(8,128)S(1)}, u32[]{:S(2)}, u32[]{:S(2)}) async-start(f32[32,32,128]{2,1,0:T(8,128)} %broadcast_in_dim.12), calls=%async_computation.1 | async-start | bytes 1048576 | tf_op jit(solution)/shard_map/all_to_all | solution.py:309
  10.1 53.6 %copy-start.4 = (f32[1024]{0:T(1024)S(1)}, f32[1024]{0:T(1024)}, u32[]{:S(2)}) copy-start(f32[1024]{0:T(1024)} %param.9) | copy-start | bytes 12292
  10.1 53.6 %copy-start.5 = (f32[1024]{0:T(1024)S(1)}, f32[1024]{0:T(1024)}, u32[]{:S(2)}) copy-start(f32[1024]{0:T(1024)} %param.8) | copy-start | bytes 12292
  38.7 25.8 %copy-start.3 = (f32[32,32,128]{2,1,0:T(8,128)}, f32[32,32,128]{2,1,0:T(8,128)S(1)}, u32[]{:S(2)}) copy-start(f32[32,32,128]{2,1,0:T(8,128)S(1)} %all-to-all-done.1.noise_ref) | copy-start | bytes 1572868
  59.9 40.6 %all-to-all-start.2 = ((f32[32,64,128]{2,1,0:T(8,128)}), f32[32,64,128]{2,1,0:T(8,128)S(1)}, u32[]{:S(2)}, u32[]{:S(2)}) async-start(f32[32,64,128]{2,1,0:T(8,128)} %bitcast.17), calls=%async_computation.2 | async-start | bytes 2097152 | tf_op jit(solution)/shard_map/all_to_all | solution.py:311
  100.5 1.0 copy-start.2
  105.6 5.8 %copy-start.6 = (s32[32]{0:T(128)S(1)}, s32[32]{0:T(128)}, u32[]{:S(2)}) copy-start(s32[32]{0:T(128)} %counts_ref.1) | copy-start | bytes 388
  105.6 54.2 %all-to-all-start.3 = ((f32[32,128,128]{2,1,0:T(8,128)}), f32[32,128,128]{2,1,0:T(8,128)S(1)}, u32[]{:S(2)}, u32[]{:S(2)}) async-start(f32[32,128,128]{2,1,0:T(8,128)} %analyse.1), calls=%async_computation.3 | async-start | bytes 4194304 | tf_op jit(solution)/shard_map/all_to_all | solution.py:342
  159.7 1.3 copy-start.1

commit v2 on v1

--- a/solution.py
+++ b/solution.py
@@ -26,81 +26,85 @@
     return lax.broadcasted_iota(jnp.int32, (ROWS, LANES), 0)
 
 
-def forecast_kernel(slot_ref, turn_ref, part_ref, x_ref, state_ref, readings_ref, *, devices, members):
+def forecast_kernel(places_ref, runs_ref, x_ref, state_ref, readings_ref, tile_ref, *, devices, members):
+    height = x_ref.shape[0]
+    tiles = height // LANES
+    halves = tiles // ROWS
+    tile_pitch = LANES + ROWS
+    cell_pitch = tiles + ROWS
     parts = ROWS // members
-    steps = state_ref.shape[0] // devices // ROWS
-    total = devices * steps
     lane = lanes_iota()
     row = rows_iota()
-    first_lane = lane == 0
-    low_lanes = lane < 2
-    last_lane = lane == LANES - 1
-    first_part = row < members
-    last_part = row >= ROWS - members
-
-    for destination in range(devices):
-        for part in range(parts):
-            for step in range(steps):
-                tile = (destination * parts + part) * steps + step
-                begin = (destination * steps + step) * ROWS + part * members
-                state_ref[begin : begin + members, :] = x_ref[:, tile * LANES : (tile + 1) * LANES] * TIME_STEP
-
-    def load(number):
-        return state_ref[number * ROWS : (number + 1) * ROWS, :]
+
+    def group(cell):
+        return [state_ref[cell * tiles + half * ROWS : cell * tiles + (half + 1) * ROWS, :] for half in range(halves)]
+
+    for tile in range(tiles):
+        tile_ref[tile * tile_pitch : tile * tile_pitch + LANES, :] = (x_ref[tile * LANES : (tile + 1) * LANES, :] * TIME_STEP).T
+    for cell in range(LANES):
+        for half in range(halves):
+            begin = cell * tiles + half * ROWS
+            state_ref[begin : begin + ROWS, :] = tile_ref[pl.ds(half * ROWS * tile_pitch + cell, ROWS, stride=tile_pitch), :]
+
+    def next_run(values):
+        turned = [pltpu.roll(value, LANES - members, axis=1) for value in values]
+        down = [pltpu.roll(value, ROWS - 1, axis=0) for value in turned]
+        carried = [jnp.where(row == ROWS - 1, down[(half + 1) % halves], down[half]) for half in range(halves)]
+        return [jnp.where(lane >= LANES - members, carry, value) for carry, value in zip(carried, turned, strict=True)]
+
+    def previous_run(values):
+        turned = [pltpu.roll(value, members, axis=1) for value in values]
+        up = [pltpu.roll(value, 1, axis=0) for value in turned]
+        carried = [jnp.where(row == 0, up[half - 1], up[half]) for half in range(halves)]
+        return [jnp.where(lane < members, carry, value) for carry, value in zip(carried, turned, strict=True)]
+
+    def advance(left_two, left, current, right):
+        return [
+            (c * (1.0 - TIME_STEP) + FORCING * TIME_STEP * TIME_STEP) + (d - a) * b
+            for a, b, c, d in zip(left_two, left, current, right, strict=True)
+        ]
+
+    def store(cell, values):
+        for half in range(halves):
+            begin = cell * tiles + half * ROWS
+            state_ref[begin : begin + ROWS, :] = values[half]
 
     def substep(_, carry):
-        wrap_first = pltpu.roll(load(0), ROWS - members, axis=0)
-        below = pltpu.roll(load(total - 1), members, axis=0)
-        for destination in range(devices):
-            start = destination * steps
-            own_last = pltpu.roll(load(start + steps - 1), members, axis=0)
-            previous = jnp.where(first_part, below, own_last)
-            below = own_last
-            if destination == 0:
-                own_first = wrap_first
-            else:
-                own_first = next_first
-            if destination + 1 < devices:
-                next_first = pltpu.roll(load(start + steps), ROWS - members, axis=0)
-            else:
-                next_first = wrap_first
-            following = jnp.where(last_part, next_first, own_first)
-            previous_one = pltpu.roll(previous, 1, axis=1)
-            previous_two = pltpu.roll(previous, 2, axis=1)
-            current = load(start)
-            current_up = pltpu.roll(current, LANES - 1, axis=1)
-            for step in range(steps):
-                after = load(start + step + 1) if step + 1 < steps else following
-                after_up = pltpu.roll(after, LANES - 1, axis=1)
-                one = pltpu.roll(current, 1, axis=1)
-                two = pltpu.roll(current, 2, axis=1)
-                left = jnp.where(first_lane, previous_one, one)
-                left_two = jnp.where(low_lanes, previous_two, two)
-                right = jnp.where(last_lane, after_up, current_up)
-                updated = (current * (1.0 - TIME_STEP) + FORCING * TIME_STEP * TIME_STEP) + (right - left_two) * left
-                begin = (start + step) * ROWS
-                state_ref[begin : begin + ROWS, :] = updated
-                previous_one, previous_two = one, two
-                current, current_up = after, after_up
+        before_two = previous_run(group(LANES - 2))
+        before = previous_run(group(LANES - 1))
+        first = [group(cell) for cell in range(3)]
+        beyond = next_run(first[0])
+        window = list(first)
+        for cell in range(2, LANES - 1):
+            right = group(cell + 1)
+            store(cell, advance(*window, right))
+            window = window[1:] + [right]
+        store(LANES - 1, advance(*window, beyond))
+        store(0, advance(before_two, before, first[0], first[1]))
+        store(1, advance(before, first[0], first[1], first[2]))
         return carry
 
     lax.fori_loop(0, PREDICT_SUBTICKS, substep, 0)
 
-    for number in range(total):
-        begin = number * ROWS
-        state_ref[begin : begin + ROWS, :] = load(number) * (1.0 / TIME_STEP)
+    for cell in range(LANES):
+        for half in range(halves):
+            begin = cell * cell_pitch + half * ROWS
+            tile_ref[begin : begin + ROWS, :] = group(cell)[half]
+    for tile in range(tiles):
+        state_ref[tile * LANES : (tile + 1) * LANES, :] = tile_ref[pl.ds(tile, LANES, stride=cell_pitch), :].T * (1.0 / TIME_STEP)
 
     def gather(block, carry):
         base = block * LANES
         picked = [jnp.zeros((ROWS, LANES), jnp.float32) for _ in range(4)]
         for number in range(LANES):
-            begin = pl.multiple_of(slot_ref[base + number] * ROWS, ROWS)
-            turned = pltpu.roll(state_ref[pl.ds(begin, ROWS), :], turn_ref[base + number], axis=1)
+            place = places_ref[base + number]
+            begin = pl.multiple_of((place // (LANES * parts)) * ROWS, ROWS)
+            turned = pltpu.roll(state_ref[pl.ds(begin, ROWS), :], (number - place) & (LANES - 1), axis=1)
             picked[number % 4] = jnp.where(lane == number, turned, picked[number % 4])
         both = picked[0]
         for number in range(1, 4):
             both = jnp.where(lane % 4 == number, picked[number], both)
-        part_of = part_ref[pl.ds(block, 1), :]
+        part_of = (runs_ref[pl.ds(block, 1), :] // LANES) % parts
         chosen = both
         for part in range(1, parts):
             chosen = jnp.where(part_of == part, pltpu.roll(both, ROWS - part * members, axis=0), chosen)
@@ -108,11 +112,18 @@
             readings_ref[destination, pl.ds(block * members, members), :] = chosen[:members]
         return carry
 
-    lax.fori_loop(0, part_ref.shape[0], gather, 0)
+    lax.fori_loop(0, runs_ref.shape[0], gather, 0)
 
 
 def dot(a, b, contract, precision=HIGH):
     return lax.dot_general(a, b, (contract, ((), ())), precision=precision, preferred_element_type=jnp.float32)
+
+
+def split_three(value):
+    high = value.astype(jnp.bfloat16)
+    rest = value - high.astype(jnp.float32)
+    middle = rest.astype(jnp.bfloat16)
+    return high, middle, (rest - middle.astype(jnp.float32)).astype(jnp.bfloat16)
 
 
 def invert_all(matrix_ref):
@@ -120,37 +131,41 @@
     lane = lanes_iota()
     row = rows_iota()
 
-    def column(value, index):
-        return jnp.take_along_axis(value, jnp.full((ROWS, LANES), index, jnp.int32), axis=1)
-
     def panel(number, carry):
         base = number * ROWS
         start = pl.multiple_of(base, ROWS)
-        inside = (lane >= base) & (lane < base + ROWS)
-        unit = jnp.where(lane - base == row, 1.0, 0.0)
-        finished = []
+        offset = lane - base
+        inside = (offset >= 0) & (offset < ROWS)
+        unit = jnp.where(offset == row, 1.0, 0.0)
+        blocks = [matrix_ref[region, pl.ds(start, ROWS), :] for region in range(regions)]
+        columns = []
+        for k in range(ROWS):
+            index = jnp.full((ROWS, LANES), base + k, jnp.int32)
+            columns.append([jnp.take_along_axis(block, index, axis=1) for block in blocks])
+        lefts = []
+        for block in blocks:
+            signed = jnp.where(inside, 0.0, jnp.where(offset < 0, block, -block))
+            high, middle, low = split_three(signed)
+            lefts.append(jnp.concatenate([high, high, middle, high, low, middle], axis=0))
+        blocks = [jnp.where(inside, unit, block) for block in blocks]
+        for j in range(ROWS):
+            here = row == j
+            for region in range(regions):
+                pivot = columns[j][region]
+                inverse = 1.0 / pivot[j : j + 1, :]
+                scaled = blocks[region][j : j + 1, :] * inverse
+                blocks[region] = jnp.where(here, scaled, blocks[region] - pivot * scaled)
+                for k in range(j + 1, ROWS):
+                    scaled = columns[k][region][j : j + 1, :] * inverse
+                    columns[k][region] = jnp.where(here, scaled, columns[k][region] - pivot * scaled)
         for region in range(regions):
-            block = matrix_ref[region, pl.ds(start, ROWS), :]
-            columns = [column(block, base + k) for k in range(ROWS)]
-            block = jnp.where(inside, unit, block)
-            for j in range(ROWS):
-                inverse = 1.0 / columns[j][j : j + 1, :]
-                here = row == j
-                scaled = block[j : j + 1, :] * inverse
-                block = jnp.where(here, scaled, block - columns[j] * scaled)
-                for k in range(j + 1, ROWS):
-                    scaled = columns[k][j : j + 1, :] * inverse
-                    columns[k] = jnp.where(here, scaled, columns[k] - columns[j] * scaled)
-            finished.append(block)
-        for region in range(regions):
-            block = finished[region]
+            high, middle, low = split_three(blocks[region])
+            right = jnp.concatenate([high, middle, high, low, high, middle], axis=0)
+            update = dot(lefts[region], right, ((0,), (0,)), lax.Precision.DEFAULT)
             for i in range(size // ROWS):
-                other = matrix_ref[region, i * ROWS : (i + 1) * ROWS, :]
-                result = jnp.where(inside, 0.0, other)
-                for k in range(ROWS):
-                    result = result - column(other, base + k) * block[k : k + 1, :]
-                matrix_ref[region, i * ROWS : (i + 1) * ROWS, :] = result
-            matrix_ref[region, pl.ds(start, ROWS), :] = block
+                rows = slice(i * ROWS, (i + 1) * ROWS)
+                matrix_ref[region, rows, :] = jnp.where(inside, 0.0, matrix_ref[region, rows, :]) + update[rows]
+            matrix_ref[region, pl.ds(start, ROWS), :] = blocks[region]
         return carry
 
     lax.fori_loop(0, size // ROWS, panel, 0)
@@ -213,19 +228,14 @@
     sources, height, _ = cells_ref.shape
     regions, total, _ = transform_ref.shape
     members = total // sources
-    parts = ROWS // members
-    steps = height // ROWS
-    tiles = parts * steps
+    tiles = height // members
     wide = tiles // regions
-    for part in range(parts):
-        for step in range(steps):
-            tile = part * steps + step
-            region, place = tile // wide, tile % wide
-            begin = step * ROWS + part * members
-            for source in range(sources):
-                block_ref[region, source * members : (source + 1) * members, place * LANES : (place + 1) * LANES] = cells_ref[
-                    source, begin : begin + members, :
-                ]
+    for tile in range(tiles):
+        region, place = tile // wide, tile % wide
+        for source in range(sources):
+            block_ref[region, source * members : (source + 1) * members, place * LANES : (place + 1) * LANES] = cells_ref[
+                source, tile * members : (tile + 1) * members, :
+            ]
     for region in range(regions):
         block = block_ref[region]
         anomalies = block - jnp.sum(block, axis=0, keepdims=True) * (1.0 / total)
@@ -285,30 +295,29 @@
     zones, local = neighbours.shape
     regions = zones // devices
     zone_cells = cells // zones
-    parts = ROWS // members
     share = cells // devices
-    steps = share // LANES // parts
     blocks = observations // LANES
 
-    slot = (measured_indexes // share) * steps + (measured_indexes // LANES) % steps
-    part = (measured_indexes // (LANES * steps)) % parts
-    turn = (jnp.arange(observations, dtype=jnp.int32) - measured_indexes) % LANES
+    runs = prior_sample_matrix.reshape(members, cells // LANES, LANES).transpose(1, 0, 2).reshape(-1, LANES)
+    height = runs.shape[0]
+    tiles = height // LANES
     state, readings = pl.pallas_call(
         functools.partial(forecast_kernel, devices=devices, members=members),
         out_shape=(
-            jax.ShapeDtypeStruct((devices * steps * ROWS, LANES), jnp.float32),
+            jax.ShapeDtypeStruct((height, LANES), jnp.float32),
             jax.ShapeDtypeStruct((devices, blocks * members, LANES), jnp.float32),
         ),
-        in_specs=[whole(pltpu.SMEM), whole(pltpu.SMEM), whole(), whole()],
+        in_specs=[whole(pltpu.SMEM), whole(), whole()],
         out_specs=(whole(), whole()),
+        scratch_shapes=[pltpu.VMEM((max(tiles * (LANES + ROWS), LANES * (tiles + ROWS)), LANES), jnp.float32)],
         name="forecast",
-    )(slot, turn, part.reshape(blocks, LANES), prior_sample_matrix)
+    )(measured_indexes, measured_indexes.reshape(blocks, LANES), runs)
 
     noise = perturbation.reshape(members, blocks, LANES).transpose(1, 0, 2).reshape(1, blocks * members, LANES)
     exchange = functools.partial(lax.all_to_all, axis_name=AXES, split_axis=0, concat_axis=0, tiled=True)
     noise = exchange(jnp.broadcast_to(noise, (devices, blocks * members, LANES)))
     readings = exchange(readings)
-    own_cells = exchange(state.reshape(devices, steps * ROWS, LANES))
+    own_cells = exchange(state.reshape(devices, height // devices, LANES))
 
     zone = device_index * regions
     table = jnp.stack([obs_values, obs_var, measured_indexes.astype(jnp.float32)])

time: 168 us -> 139 us (0.83)
  Pallas kernels: 75.2 us -> 38.1 us
  waiting for transfers between devices: 47.7 us -> 60.3 us
  starting transfers between devices: 16.1 us -> 13.4 us
    pallas_call x1, Pallas kernels: 36.1 us -> 13.4 us  [per_device(): pl.pallas_call(functools.partial(solve_kernel, cells=float(cells), zone_c...]
    pallas_call x1, Pallas kernels: 28.6 us -> 14.1 us  [per_device(): pl.pallas_call(functools.partial(forecast_kernel, devices=devices, member...]
    all_to_all x1, waiting for transfers between devices: 0.01 us -> 11.5 us  [per_device(): own_cells = exchange(state.reshape(devices, height // devices, LANES))]
    all_to_all x1, starting transfers between devices: 5.83 us -> 3.15 us  [per_device(): owned = exchange(outgoing).reshape(devices * tiles * CAP, LANES)]
  transfers between devices with their start and end apart: 3 -> 3, of which waited for: 1 -> 3; matrix products, arithmetic and copies ran while one was open for 2% -> 1% of each run, Pallas kernels for 39% -> 20%
where the time goes in v2:
time: 139 us; the launch traced here: 138 us
  waiting for transfers between devices  60.3 us (43%)
  Pallas kernels  38.1 us (27%)
  blocking collectives  20.1 us (14%)
  starting transfers between devices  13.4 us (10%)
  local copies, waits for them, and re-layouts  5.24 us (4%)
    all_to_all x1, waiting for transfers between devices, per_device(): owned = exchange(outgoing).reshape(devices * tiles * CAP, LANES)  47.7 us
    all_to_all x1, blocking collectives, per_device(): readings = exchange(readings)  20.1 us
    pallas_call x1, Pallas kernels, per_device(): pl.pallas_call(functools.partial(forecast_kernel, devices=devices, member...  14.1 us
    pallas_call x1, Pallas kernels, per_device(): pl.pallas_call(functools.partial(solve_kernel, cells=float(cells), zone_c...  13.4 us
    all_to_all x1, waiting for transfers between devices, per_device(): own_cells = exchange(state.reshape(devices, height // devices, LANES))  11.5 us
    all_to_all x1, starting transfers between devices, per_device(): exchange(jnp.broadcast_to(noise, (devices, blocks * members, LANES)))  7.08 us
    pallas_call x1, Pallas kernels, per_device(): pl.pallas_call(advance_kernel, grid=(chunks,), out_shape=jax.ShapeDtypeSt...  6.45 us
    pallas_call x1, Pallas kernels, per_device(): pl.pallas_call(apply_kernel, out_shape=jax.ShapeDtypeStruct((devices, til...  4.12 us
  transfers between devices with their start and end apart: 3, of which 3 were waited for; matrix products, arithmetic and copies ran while one was open for 1% of the time, Pallas kernels for 20%

profile of v2, /device:TPU:1, one launch (start us, length us, event | category | flops | bytes accessed | tf_op | source)
XLA Modules:
  0.0 137.9 jit_solution(7074544302202847343)
XLA Ops:
  0.0 0.0 copy-start
  0.0 0.8 copy.12
  0.8 0.9 broadcast_in_dim.12
  1.6 7.1 %all-to-all-start.1 = ((f32[32,32,128]{2,1,0:T(8,128)}), f32[32,32,128]{2,1,0:T(8,128)S(1)}, u32[]{:S(2)}, u32[]{:S(2)}) async-start(f32[32,32,128]{2,1,0:T(8,128)} %broadcast_in_dim.12), calls=%async_computation.1 | async-start | bytes 1048576 | tf_op jit(solution)/shard_map/all_to_all | solution.py:318
  8.7 0.0 copy-start.4
  8.7 0.0 copy-start.5
  8.7 0.0 copy-start.6
  8.7 14.1 %forecast.1 = (f32[2048,128]{1,0:T(8,128)}, f32[32,32,128]{2,1,0:T(8,128)}) custom-call(s32[1024]{0:T(1024)} %places_ref.1, s32[8,128]{1,0:T(8,128)} %bitcast.25, f32[2048,128]{1,0:T(8,128)} %bitcast.21), custom_call_target="tpu_custom_call" | custom-call | tf_op jit(solution)/shard_map/forecast/pallas_call | solution.py:304
  22.9 1.1 all-to-all-done.1.noise_ref
  24.0 20.1 %all_to_all.20.readings_ref = f32[32,32,128]{2,1,0:T(8,128)} all-to-all(f32[32,32,128]{2,1,0:T(8,128)} %get-tuple-element.7), channel_id=1, replica_groups=mesh['member'=8,'region'=4] {'member','region'}, dimensions={0} | all-to-all | bytes 1048576 | tf_op jit(solution)/shard_map/all_to_all | solution.py:319
  44.1 3.2 %all-to-all-start.2 = ((f32[32,64,128]{2,1,0:T(8,128)}), f32[32,64,128]{2,1,0:T(8,128)S(1)}, u32[]{:S(2)}, u32[]{:S(2)}) async-start(f32[32,64,128]{2,1,0:T(8,128)} %bitcast.22), calls=%async_computation.2 | async-start | bytes 2097152 | tf_op jit(solution)/shard_map/all_to_all | solution.py:320
  47.2 0.0 copy-done.4
  47.3 0.1 pad.3.clone
  47.4 0.6 constant_dynamic-slice_fusion.neighbours_ref
  47.9 0.7 maximum_maximum_fusion.table_ref
  48.6 13.4 %solve.1.transform_ref = f32[4,128,128]{2,1,0:T(8,128)} custom-call(s32[1]{0:T(128)} %bitcast.zone_ref, s32[4,128]{1,0:T(4,128)} %constant_dynamic-slice_fusion.neighbours_ref, f32[8,1024]{1,0:T(8,128)} %maximum_maximum_fusion.table_ref, f32[32,32,128]{2,1,0:T(8,128)} %all_to_all.20.readings_ref, f32[32,32,128]{2,1,0:T(8,128)} %copy-done.3), custom_call_target="tpu_custom_call" | custom-call | tf_op jit(solution)/shard_map/solve/pallas_call | solution.py:326
  62.1 11.5 %all-to-all-done.2.cells_ref = f32[32,64,128]{2,1,0:T(8,128)S(1)} async-done(((f32[32,64,128]{2,1,0:T(8,128)}), f32[32,64,128]{2,1,0:T(8,128)S(1)}, u32[]{:S(2)}, u32[]{:S(2)}) %all-to-all-start.2) | async-done | bytes 1048608 | tf_op jit(solution)/shard_map/all_to_all | solution.py:320
  73.6 1.0 copy-done.2
  74.5 4.1 %analyse.1 = f32[32,128,128]{2,1,0:T(8,128)} custom-call(s32[32]{0:T(128)} %counts_ref.1, f32[4,128,128]{2,1,0:T(8,128)} %solve.1.transform_ref, f32[32,64,128]{2,1,0:T(8,128)} %copy-done.2), custom_call_target="tpu_custom_call" | custom-call | tf_op jit(solution)/shard_map/analyse/pallas_call | solution.py:340
  78.7 3.1 %all-to-all-start.3 = ((f32[32,128,128]{2,1,0:T(8,128)}), f32[32,128,128]{2,1,0:T(8,128)S(1)}, u32[]{:S(2)}, u32[]{:S(2)}) async-start(f32[32,128,128]{2,1,0:T(8,128)} %analyse.1), calls=%async_computation.3 | async-start | bytes 4194304 | tf_op jit(solution)/shard_map/all_to_all | solution.py:351
  81.8 0.6 dynamic_slice.6.count_ref
  82.5 47.7 %all-to-all-done.3 = f32[32,128,128]{2,1,0:T(8,128)S(1)} async-done(((f32[32,128,128]{2,1,0:T(8,128)}), f32[32,128,128]{2,1,0:T(8,128)S(1)}, u32[]{:S(2)}, u32[]{:S(2)}) %all-to-all-start.3) | async-done | bytes 2097184 | tf_op jit(solution)/shard_map/all_to_all | solution.py:351
  130.1 1.3 copy-done.1
  131.5 6.4 %advance.1 = f32[8,65536]{1,0:T(8,128)} custom-call(s32[1]{0:T(128)} %dynamic_slice.6.count_ref, f32[4096,128]{1,0:T(8,128)} %bitcast.20), custom_call_target="tpu_custom_call" | custom-call | tf_op jit(solution)/shard_map/advance/pallas_call | solution.py:354
  (12 shorter events, 0.0 us)
Async XLA Ops:
  0.0 47.4 %copy-start = (s32[128,128]{1,0:T(8,128)S(1)}, s32[128,128]{1,0:T(8,128)}, u32[]{:S(2)}) copy-start(s32[128,128]{1,0:T(8,128)} %param.11) | copy-start | bytes 196612
  1.6 22.4 %all-to-all-start.1 = ((f32[32,32,128]{2,1,0:T(8,128)}), f32[32,32,128]{2,1,0:T(8,128)S(1)}, u32[]{:S(2)}, u32[]{:S(2)}) async-start(f32[32,32,128]{2,1,0:T(8,128)} %broadcast_in_dim.12), calls=%async_computation.1 | async-start | bytes 1048576 | tf_op jit(solution)/shard_map/all_to_all | solution.py:318
  8.7 38.5 %copy-start.4 = (s32[1024]{0:T(1024)S(1)}, s32[1024]{0:T(1024)}, u32[]{:S(2)}) copy-start(s32[1024]{0:T(1024)} %places_ref.1) | copy-start | bytes 12292
  8.7 39.2 %copy-start.5 = (f32[1024]{0:T(1024)S(1)}, f32[1024]{0:T(1024)}, u32[]{:S(2)}) copy-start(f32[1024]{0:T(1024)} %param.9) | copy-start | bytes 12292
  8.7 39.2 %copy-start.6 = (f32[1024]{0:T(1024)S(1)}, f32[1024]{0:T(1024)}, u32[]{:S(2)}) copy-start(f32[1024]{0:T(1024)} %param.8) | copy-start | bytes 12292
  24.0 24.6 %copy-start.3 = (f32[32,32,128]{2,1,0:T(8,128)}, f32[32,32,128]{2,1,0:T(8,128)S(1)}, u32[]{:S(2)}) copy-start(f32[32,32,128]{2,1,0:T(8,128)S(1)} %all-to-all-done.1.noise_ref) | copy-start | bytes 1572868
  44.1 29.5 %all-to-all-start.2 = ((f32[32,64,128]{2,1,0:T(8,128)}), f32[32,64,128]{2,1,0:T(8,128)S(1)}, u32[]{:S(2)}, u32[]{:S(2)}) async-start(f32[32,64,128]{2,1,0:T(8,128)} %bitcast.22), calls=%async_computation.2 | async-start | bytes 2097152 | tf_op jit(solution)/shard_map/all_to_all | solution.py:320
  73.6 1.0 copy-start.2
  78.7 3.2 %copy-start.7 = (s32[32]{0:T(128)S(1)}, s32[32]{0:T(128)}, u32[]{:S(2)}) copy-start(s32[32]{0:T(128)} %counts_ref.1) | copy-start | bytes 388
  78.7 51.5 %all-to-all-start.3 = ((f32[32,128,128]{2,1,0:T(8,128)}), f32[32,128,128]{2,1,0:T(8,128)S(1)}, u32[]{:S(2)}, u32[]{:S(2)}) async-start(f32[32,128,128]{2,1,0:T(8,128)} %analyse.1), calls=%async_computation.3 | async-start | bytes 4194304 | tf_op jit(solution)/shard_map/all_to_all | solution.py:351
  130.1 1.3 copy-start.1

commit v3 on v2

v3 whole, which is shorter than its diff:
```python
import functools

import jax
import jax.numpy as jnp
from jax import lax
from jax.experimental import pallas as pl
from jax.experimental.pallas import tpu as pltpu
from jax.sharding import PartitionSpec as P

PREDICT_SUBTICKS = 24
CAP = 8
LSCALE = 2048
FORCING = 8.0
TIME_STEP = 0.01
HIGH = lax.Precision.HIGHEST
AXES = ("member", "region")
LANES = 128
ROWS = 8


def lanes_iota():
    return lax.broadcasted_iota(jnp.int32, (ROWS, LANES), 1)


def rows_iota():
    return lax.broadcasted_iota(jnp.int32, (ROWS, LANES), 0)


def forecast_kernel(places_ref, x_ref, *refs, devices, members):
    *chunk_refs, readings_ref, state_ref, tile_ref, table_ref, scalar_ref, table_sem = refs
    height = x_ref.shape[0]
    blocks = places_ref.shape[0]
    tiles = height // LANES
    halves = tiles // ROWS
    tile_pitch = LANES + ROWS
    cell_pitch = tiles + ROWS
    parts = ROWS // members
    lane = lanes_iota()
    row = rows_iota()

    def group(cell):
        return [state_ref[cell * tiles + half * ROWS : cell * tiles + (half + 1) * ROWS, :] for half in range(halves)]

    for tile in range(tiles):
        tile_ref[tile * tile_pitch : tile * tile_pitch + LANES, :] = (x_ref[tile * LANES : (tile + 1) * LANES, :] * TIME_STEP).T
    for cell in range(LANES):
        for half in range(halves):
            begin = cell * tiles + half * ROWS
            state_ref[begin : begin + ROWS, :] = tile_ref[pl.ds(half * ROWS * tile_pitch + cell, ROWS, stride=tile_pitch), :]

    places = places_ref[...]
    column = lax.broadcasted_iota(jnp.int32, places.shape, 1)
    table_ref[:blocks, :] = (places // (LANES * parts)) * ROWS
    table_ref[blocks:, :] = (column - places) & (LANES - 1)
    table_copy = pltpu.make_async_copy(table_ref, scalar_ref, table_sem)
    table_copy.start()

    def next_run(values):
        turned = [pltpu.roll(value, LANES - members, axis=1) for value in values]
        down = [pltpu.roll(value, ROWS - 1, axis=0) for value in turned]
        carried = [jnp.where(row == ROWS - 1, down[(half + 1) % halves], down[half]) for half in range(halves)]
        return [jnp.where(lane >= LANES - members, carry, value) for carry, value in zip(carried, turned, strict=True)]

    def previous_run(values):
        turned = [pltpu.roll(value, members, axis=1) for value in values]
        up = [pltpu.roll(value, 1, axis=0) for value in turned]
        carried = [jnp.where(row == 0, up[half - 1], up[half]) for half in range(halves)]
        return [jnp.where(lane < members, carry, value) for carry, value in zip(carried, turned, strict=True)]

    def advance(left_two, left, current, right):
        return [
            (c * (1.0 - TIME_STEP) + FORCING * TIME_STEP * TIME_STEP) + (d - a) * b
            for a, b, c, d in zip(left_two, left, current, right, strict=True)
        ]

    def store(cell, values):
        for half in range(halves):
            begin = cell * tiles + half * ROWS
            state_ref[begin : begin + ROWS, :] = values[half]

    def substep(_, carry):
        before_two = previous_run(group(LANES - 2))
        before = previous_run(group(LANES - 1))
        first = [group(cell) for cell in range(3)]
        beyond = next_run(first[0])
        window = list(first)
        for cell in range(2, LANES - 1):
            right = group(cell + 1)
            store(cell, advance(*window, right))
            window = window[1:] + [right]
        store(LANES - 1, advance(*window, beyond))
        store(0, advance(before_two, before, first[0], first[1]))
        store(1, advance(before, first[0], first[1], first[2]))
        return carry

    lax.fori_loop(0, PREDICT_SUBTICKS, substep, 0)

    for cell in range(LANES):
        for half in range(halves):
            begin = cell * cell_pitch + half * ROWS
            tile_ref[begin : begin + ROWS, :] = group(cell)[half]
    for tile in range(tiles):
        state_ref[tile * LANES : (tile + 1) * LANES, :] = tile_ref[pl.ds(tile, LANES, stride=cell_pitch), :].T * (1.0 / TIME_STEP)
    share = height // devices
    part_rows = share // len(chunk_refs)
    for destination in range(devices):
        for number, chunk_ref in enumerate(chunk_refs):
            begin = destination * share + number * part_rows
            chunk_ref[destination, :, :] = state_ref[begin : begin + part_rows, :]
    table_copy.wait()

    def gather(block, carry):
        picked = [jnp.zeros((ROWS, LANES), jnp.float32) for _ in range(4)]
        for number in range(LANES):
            begin = pl.multiple_of(scalar_ref[block, number], ROWS)
            turned = pltpu.roll(state_ref[pl.ds(begin, ROWS), :], scalar_ref[blocks + block, number], axis=1)
            picked[number % 4] = jnp.where(lane == number, turned, picked[number % 4])
        both = picked[0]
        for number in range(1, 4):
            both = jnp.where(lane % 4 == number, picked[number], both)
        part_of = (places_ref[pl.ds(block, 1), :] // LANES) % parts
        chosen = both
        for part in range(1, parts):
            chosen = jnp.where(part_of == part, pltpu.roll(both, ROWS - part * members, axis=0), chosen)
        for destination in range(devices):
            readings_ref[destination, pl.ds(block * members, members), :] = chosen[:members]
        return carry

    lax.fori_loop(0, blocks, gather, 0)


def dot(a, b, contract, precision=HIGH):
    return lax.dot_general(a, b, (contract, ((), ())), precision=precision, preferred_element_type=jnp.float32)


def split_three(value):
    high = value.astype(jnp.bfloat16)
    rest = value - high.astype(jnp.float32)
    middle = rest.astype(jnp.bfloat16)
    return high, middle, (rest - middle.astype(jnp.float32)).astype(jnp.bfloat16)


def invert_all(matrix_ref):
    regions, size, _ = matrix_ref.shape
    lane = lanes_iota()
    row = rows_iota()

    def panel(number, carry):
        base = number * ROWS
        start = pl.multiple_of(base, ROWS)
        offset = lane - base
        inside = (offset >= 0) & (offset < ROWS)
        unit = jnp.where(offset == row, 1.0, 0.0)
        blocks = [matrix_ref[region, pl.ds(start, ROWS), :] for region in range(regions)]
        columns = []
        for k in range(ROWS):
            index = jnp.full((ROWS, LANES), base + k, jnp.int32)
            columns.append([jnp.take_along_axis(block, index, axis=1) for block in blocks])
        lefts = []
        for block in blocks:
            signed = jnp.where(inside, 0.0, jnp.where(offset < 0, block, -block))
            high, middle, low = split_three(signed)
            lefts.append(jnp.concatenate([high, high, middle, high, low, middle], axis=0))
        blocks = [jnp.where(inside, unit, block) for block in blocks]
        for j in range(ROWS):
            here = row == j
            for region in range(regions):
                pivot = columns[j][region]
                inverse = 1.0 / pivot[j : j + 1, :]
                scaled = blocks[region][j : j + 1, :] * inverse
                blocks[region] = jnp.where(here, scaled, blocks[region] - pivot * scaled)
                for k in range(j + 1, ROWS):
                    scaled = columns[k][region][j : j + 1, :] * inverse
                    columns[k][region] = jnp.where(here, scaled, columns[k][region] - pivot * scaled)
        for region in range(regions):
            high, middle, low = split_three(blocks[region])
            right = jnp.concatenate([high, middle, high, low, high, middle], axis=0)
            update = dot(lefts[region], right, ((0,), (0,)), lax.Precision.DEFAULT)
            for i in range(size // ROWS):
                rows = slice(i * ROWS, (i + 1) * ROWS)
                matrix_ref[region, rows, :] = jnp.where(inside, 0.0, matrix_ref[region, rows, :]) + update[rows]
            matrix_ref[region, pl.ds(start, ROWS), :] = blocks[region]
        return carry

    lax.fori_loop(0, size // ROWS, panel, 0)


def store_pieces(pieces_ref, value):
    height = value.shape[0]
    for number, piece in enumerate(split_three(value)):
        pieces_ref[number * height : (number + 1) * height, :] = piece


def select(pieces_ref, pick):
    height = pieces_ref.shape[0] // 3
    picked = dot(pieces_ref[...], pick, ((1,), (0,)), lax.Precision.DEFAULT)
    return picked[:height] + picked[height : 2 * height] + picked[2 * height :]


def spread_rows(stack_ref, source_ref, offset, members, convert):
    sources, height, _ = source_ref.shape
    for block in range(height // members):
        lanes = slice(block * LANES, (block + 1) * LANES)
        for source in range(sources):
            begin = offset + source * members
            stack_ref[begin : begin + members, lanes] = convert(lanes, source_ref[source, block * members : (block + 1) * members, :])


def prepare_kernel(zone_ref, neighbours_ref, table_ref, noise_ref, pick_ref, errors_ref, target_ref, stack_ref, pieces_ref, *, cells, zone_cells):
    regions, total, _ = target_ref.shape
    members = total // noise_ref.shape[0]
    observations = table_ref.shape[1]
    size = neighbours_ref.shape[1]
    spread_rows(
        stack_ref,
        noise_ref,
        0,
        members,
        lambda lanes, noise: table_ref[0:1, lanes] + jnp.sqrt(table_ref[1:2, lanes]) * noise,
    )
    stack_ref[total : total + ROWS, :] = table_ref[...]
    stack_ref[total + ROWS :, :] = jnp.zeros((ROWS, observations), jnp.float32)
    store_pieces(pieces_ref, stack_ref[...])
    ids = lax.broadcasted_iota(jnp.int32, (observations, size), 0)
    for region in range(regions):
        pick = jnp.where(ids == neighbours_ref[region : region + 1, :], 1.0, 0.0).astype(jnp.bfloat16)
        pick_ref[region, :, :] = pick
        picked = select(pieces_ref, pick)
        target_ref[region, :, :] = picked[:total]
        variance = picked[total + 1 : total + 2]
        place = picked[total + 2 : total + 3]
        centre = ((zone_ref[0] + region) * zone_cells + zone_cells // 2).astype(jnp.float32)
        gap = jnp.abs(place - centre)
        scaled = jnp.minimum(gap, cells - gap) / float(LSCALE)
        errors_ref[region : region + 1, :] = variance * (1.0 + scaled * scaled)


def solve_kernel(pick_ref, errors_ref, target_ref, readings_ref, transform_ref, stack_ref, pieces_ref, matrix_ref):
    regions, total, _ = transform_ref.shape
    members = total // readings_ref.shape[0]
    size = pick_ref.shape[2]
    spread_rows(stack_ref, readings_ref, 0, members, lambda lanes, value: value)
    store_pieces(pieces_ref, stack_ref[...])
    diagonal = lax.broadcasted_iota(jnp.int32, (size, size), 0) == lax.broadcasted_iota(jnp.int32, (size, size), 1)
    anomalies, innovations = [], []
    for region in range(regions):
        equivalents = select(pieces_ref, pick_ref[region])
        innovations.append(target_ref[region] - equivalents)
        anomaly = equivalents - jnp.sum(equivalents, axis=0, keepdims=True) * (1.0 / total)
        anomalies.append(anomaly)
        covariance = dot(anomaly, anomaly, ((0,), (0,))) * (1.0 / (total - 1))
        matrix_ref[region, :, :] = jnp.where(diagonal, covariance + errors_ref[region : region + 1, :], covariance)
    invert_all(matrix_ref)
    for region in range(regions):
        weights = dot(innovations[region], matrix_ref[region], ((1,), (0,)))
        transform_ref[region, :, :] = dot(weights, anomalies[region], ((1,), (1,))) * (1.0 / (total - 1))


def apply_kernel(counts_ref, transform_ref, cells_ref, owned_ref, block_ref, result_ref, *, first, wide):
    sources, height, _ = cells_ref.shape
    _, total, _ = transform_ref.shape
    members = total // sources
    tiles = height // members
    for tile in range(tiles):
        lanes = slice(tile * LANES, (tile + 1) * LANES)
        for source in range(sources):
            block_ref[source * members : (source + 1) * members, lanes] = cells_ref[source, tile * members : (tile + 1) * members, :]
    tile = 0
    while tile < tiles:
        region = (first + tile) // wide
        until = min(tiles, (region + 1) * wide - first)
        block = block_ref[:, tile * LANES : until * LANES]
        anomalies = block - jnp.sum(block, axis=0, keepdims=True) * (1.0 / total)
        analysed = block + dot(transform_ref[region], anomalies, ((1,), (0,)))
        for number in range(tile, until):
            result_ref[number, :total, :] = analysed[:, (number - tile) * LANES : (number - tile + 1) * LANES]
        tile = until
    for tile in range(tiles):
        result_ref[tile, total:, :] = jnp.zeros((ROWS, LANES), jnp.float32)

    def window(destination, offset):
        for tile in range(tiles):
            owned_ref[destination, tile * ROWS : (tile + 1) * ROWS, :] = result_ref[tile, pl.ds(offset, CAP), :]
        return offset + counts_ref[destination]

    lax.fori_loop(0, sources, window, jnp.int32(0))


def advance_kernel(count_ref, *refs):
    *chunk_refs, out_ref = refs
    sources, height, _ = chunk_refs[0].shape
    share = height // ROWS
    tiles = share * len(chunk_refs)
    here = out_ref.shape[1] // LANES // tiles
    lane = lanes_iota()
    occupied = rows_iota() < count_ref[0]
    start = pl.program_id(0) * here

    def load(source, tile):
        return chunk_refs[tile // share][source, (tile % share) * ROWS : (tile % share + 1) * ROWS, :]

    before = load(lax.rem(start + sources - 1, sources), tiles - 1)
    before_one = pltpu.roll(before, 1, axis=1)
    before_two = pltpu.roll(before, 2, axis=1)
    current = load(start, 0)
    current_up = pltpu.roll(current, LANES - 1, axis=1)
    for number in range(here * tiles):
        source, tile = divmod(number + 1, tiles)
        after = load(start + source if source < here else lax.rem(start + here, sources), tile)
        after_up = pltpu.roll(after, LANES - 1, axis=1)
        one = pltpu.roll(current, 1, axis=1)
        two = pltpu.roll(current, 2, axis=1)
        left = jnp.where(lane == 0, before_one, one)
        left_two = jnp.where(lane < 2, before_two, two)
        right = jnp.where(lane == LANES - 1, after_up, current_up)
        stepped = current + TIME_STEP * ((right - left_two) * left - current + FORCING)
        out_ref[:, number * LANES : (number + 1) * LANES] = jnp.where(occupied, stepped, 0.0)
        before_one, before_two = one, two
        current, current_up = after, after_up


def whole(space=pltpu.VMEM):
    return pl.BlockSpec(memory_space=space)


CHUNKS = 1


def in_vmem(value):
    return pltpu.with_memory_space_constraint(value, pltpu.VMEM)


def per_device(prior_sample_matrix, obs_values, obs_var, measured_indexes, neighbours, perturbation, counts):
    devices = lax.axis_size(AXES)
    device_index = lax.axis_index(AXES)
    members, cells = prior_sample_matrix.shape
    total = members * devices
    observations = obs_values.shape[0]
    zones, local = neighbours.shape
    regions = zones // devices
    zone_cells = cells // zones
    blocks = observations // LANES
    share_tiles = cells // devices // LANES
    chunk_tiles = share_tiles // CHUNKS
    exchange = functools.partial(lax.all_to_all, axis_name=AXES, split_axis=0, concat_axis=0, tiled=True)

    def by_block(value):
        return value.reshape(devices, members, blocks, LANES).transpose(0, 2, 1, 3).reshape(devices, blocks * members, LANES)

    noise = by_block(exchange(jnp.broadcast_to(perturbation[None], (devices, members, observations))))

    runs = prior_sample_matrix.reshape(members, cells // LANES, LANES).transpose(1, 0, 2).reshape(-1, LANES)
    height = runs.shape[0]
    tiles = height // LANES
    chunk_shape = jax.ShapeDtypeStruct((devices, chunk_tiles * members, LANES), jnp.float32)
    *states, readings = pl.pallas_call(
        functools.partial(forecast_kernel, devices=devices, members=members),
        out_shape=(chunk_shape,) * CHUNKS + (jax.ShapeDtypeStruct((devices, blocks * members, LANES), jnp.float32),),
        in_specs=[whole(), whole()],
        out_specs=(whole(),) * (CHUNKS + 1),
        scratch_shapes=[
            pltpu.VMEM((height, LANES), jnp.float32),
            pltpu.VMEM((max(tiles * (LANES + ROWS), LANES * (tiles + ROWS)), LANES), jnp.float32),
            pltpu.VMEM((2 * blocks, LANES), jnp.int32),
            pltpu.SMEM((2 * blocks, LANES), jnp.int32),
            pltpu.SemaphoreType.DMA,
        ],
        name="forecast",
    )(measured_indexes.reshape(blocks, LANES), runs)

    readings = exchange(readings)
    own_cells = [exchange(state) for state in states]

    zone = device_index * regions
    table = jnp.stack([obs_values, obs_var, measured_indexes.astype(jnp.float32)])
    table = jnp.concatenate([table, jnp.zeros((ROWS - 3, observations), jnp.float32)])
    pick, errors, target = pl.pallas_call(
        functools.partial(prepare_kernel, cells=float(cells), zone_cells=zone_cells),
        out_shape=(
            jax.ShapeDtypeStruct((regions, observations, local), jnp.bfloat16),
            jax.ShapeDtypeStruct((regions, local), jnp.float32),
            jax.ShapeDtypeStruct((regions, total, local), jnp.float32),
        ),
        in_specs=[whole(pltpu.SMEM), whole(), whole(), whole()],
        out_specs=(whole(),) * 3,
        scratch_shapes=[
            pltpu.VMEM((total + 2 * ROWS, observations), jnp.float32),
            pltpu.VMEM((3 * (total + 2 * ROWS), observations), jnp.bfloat16),
        ],
        name="prepare",
    )(zone.reshape(1), lax.dynamic_slice_in_dim(neighbours, zone, regions, 0), table, in_vmem(noise))
    transform = pl.pallas_call(
        solve_kernel,
        out_shape=jax.ShapeDtypeStruct((regions, total, total), jnp.float32),
        in_specs=[whole()] * 4,
        out_specs=whole(),
        scratch_shapes=[
            pltpu.VMEM((total, observations), jnp.float32),
            pltpu.VMEM((3 * total, observations), jnp.bfloat16),
            pltpu.VMEM((regions, local, local), jnp.float32),
        ],
        name="solve",
    )(pick, errors, target, in_vmem(readings))
    transform = in_vmem(transform)

    owned = []
    for number in range(CHUNKS):
        outgoing = pl.pallas_call(
            functools.partial(apply_kernel, first=number * chunk_tiles, wide=zone_cells // LANES),
            out_shape=jax.ShapeDtypeStruct((devices, chunk_tiles * CAP, LANES), jnp.float32),
            in_specs=[whole(pltpu.SMEM), whole(), whole()],
            out_specs=whole(),
            scratch_shapes=[
                pltpu.VMEM((total, chunk_tiles * LANES), jnp.float32),
                pltpu.VMEM((chunk_tiles, total + ROWS, LANES), jnp.float32),
            ],
            name=f"analyse{number}",
        )(counts, transform, in_vmem(own_cells[number]))
        owned.append(in_vmem(exchange(outgoing)))

    steps = 8
    return pl.pallas_call(
        advance_kernel,
        grid=(steps,),
        out_shape=jax.ShapeDtypeStruct((CAP, cells), jnp.float32),
        in_specs=[whole(pltpu.SMEM)] + [whole()] * CHUNKS,
        out_specs=pl.BlockSpec((CAP, cells // steps), lambda i: (0, i)),
        name="advance",
    )(lax.dynamic_slice_in_dim(counts, device_index, 1, 0), *owned)


def solution(mesh):
    rows = P(AXES, None)
    return jax.shard_map(
        per_device, mesh=mesh, in_specs=(rows, P(), P(), P(), P(), rows, P()), out_specs=rows, check_vma=False
    )
```

time: 139 us -> 133 us (0.957)
  Pallas kernels: 38.1 us -> 32.5 us
  waiting for transfers between devices: 60.3 us -> 63.6 us
  blocking collectives: 20.1 us -> 18.4 us
    pallas_call x1, Pallas kernels: 14.1 us -> 9.85 us  [per_device(): pl.pallas_call(functools.partial(forecast_kernel, devices=devices, member...]
    all_to_all x3, waiting for transfers between devices: 60.3 us -> 63.6 us  [the longest x1 47.7 us: per_device(): owned.append(in_vmem(exchange(outgoing)))]
    unnamed x17 -> x12, local copies, waits for them, and re-layouts: 3.1 us -> 0.98 us
    all_to_all x1, blocking collectives: 20.1 us -> 18.4 us  [per_device(): readings = exchange(readings)]
    pallas_call x3 -> x4, Pallas kernels: 24 us -> 22.7 us  [the longest x1 11.7 us: per_device(): pl.pallas_call(solve_kernel, out_shape=jax.ShapeDtypeStruct((regions, tot...]
  transfers between devices with their start and end apart: 3 -> 3, of which waited for: 3 -> 3; matrix products, arithmetic and copies ran while one was open for 1% -> 1% of each run, Pallas kernels for 20% -> 18%
where the time goes in v3:
time: 133 us
  waiting for transfers between devices  63.6 us (48%)
  Pallas kernels  32.5 us (24%)
  blocking collectives  18.4 us (14%)
  starting transfers between devices  13.4 us (10%)
  local copies, waits for them, and re-layouts  3.88 us (3%)
    all_to_all x1, waiting for transfers between devices, per_device(): owned.append(in_vmem(exchange(outgoing)))  47.7 us
    all_to_all x1, blocking collectives, per_device(): readings = exchange(readings)  18.4 us
    pallas_call x1, Pallas kernels, per_device(): pl.pallas_call(solve_kernel, out_shape=jax.ShapeDtypeStruct((regions, tot...  11.7 us
    all_to_all x1, waiting for transfers between devices, per_device(): own_cells = [exchange(state) for state in states]  10.6 us
    pallas_call x1, Pallas kernels, per_device(): pl.pallas_call(functools.partial(forecast_kernel, devices=devices, member...  9.85 us
    all_to_all x1, starting transfers between devices, per_device(): exchange(jnp.broadcast_to(perturbation[None], (devices, members, observat...  7.08 us
    all_to_all x1, waiting for transfers between devices, per_device(): exchange(jnp.broadcast_to(perturbation[None], (devices, members, observat...  5.37 us
    pallas_call x1, Pallas kernels, per_device(): pl.pallas_call(advance_kernel, grid=(steps,), out_shape=jax.ShapeDtypeStr...  4.81 us
  transfers between devices with their start and end apart: 3, of which 3 were waited for; matrix products, arithmetic and copies ran while one was open for 1% of the time, Pallas kernels for 18%

profile of v3, /device:TPU:1, one launch (start us, length us, event | category | flops | bytes accessed | tf_op | source)
XLA Modules:
  0.0 132.6 jit_solution(1255127256466487412)
XLA Ops:
  0.0 0.0 copy-start
  0.0 1.7 %broadcast_in_dim.10 = f32[32,4,1024]{2,1,0:T(4,128)} broadcast(f32[4,1024]{1,0:T(4,128)} %param.12), dimensions={1,2} | broadcast | bytes 540672 | tf_op jit(solution)/shard_map/broadcast_in_dim | solution.py:350
  1.7 7.1 %all-to-all-start = ((f32[32,4,1024]{2,1,0:T(4,128)}), f32[32,4,1024]{2,1,0:T(4,128)S(1)}, u32[]{:S(2)}, u32[]{:S(2)}) async-start(f32[32,4,1024]{2,1,0:T(4,128)} %broadcast_in_dim.10), calls=%async_computation | async-start | bytes 1048576 | tf_op jit(solution)/shard_map/all_to_all | solution.py:350
  8.8 0.0 copy-start.2
  8.8 0.0 copy-start.3
  8.8 0.0 copy-start.4
  8.8 9.9 %forecast.1 = (f32[32,64,128]{2,1,0:T(8,128)}, f32[32,32,128]{2,1,0:T(8,128)}) custom-call(s32[8,128]{1,0:T(8,128)} %bitcast.17, f32[2048,128]{1,0:T(8,128)} %bitcast.16), custom_call_target="tpu_custom_call" | custom-call | tf_op jit(solution)/shard_map/forecast/pallas_call | solution.py:356
  18.7 5.4 %all-to-all-done = f32[32,4,1024]{2,1,0:T(4,128)S(1)} async-done(((f32[32,4,1024]{2,1,0:T(4,128)}), f32[32,4,1024]{2,1,0:T(4,128)S(1)}, u32[]{:S(2)}, u32[]{:S(2)}) %all-to-all-start) | async-done | bytes 524320 | tf_op jit(solution)/shard_map/all_to_all | solution.py:350
  24.0 18.4 %all_to_all.20.readings_ref = f32[32,32,128]{2,1,0:T(8,128)S(1)} all-to-all(f32[32,32,128]{2,1,0:T(8,128)} %get-tuple-element.13), channel_id=1, replica_groups=mesh['member'=8,'region'=4] {'member','region'}, dimensions={0} | all-to-all | bytes 1048576 | tf_op jit(solution)/shard_map/all_to_all | solution.py:371
  42.4 3.2 %all-to-all-start.2 = ((f32[32,64,128]{2,1,0:T(8,128)}), f32[32,64,128]{2,1,0:T(8,128)S(1)}, u32[]{:S(2)}, u32[]{:S(2)}) async-start(f32[32,64,128]{2,1,0:T(8,128)} %get-tuple-element.14), calls=%async_computation.2 | async-start | bytes 2097152 | tf_op jit(solution)/shard_map/all_to_all | solution.py:372
  45.6 0.0 copy-done.2
  45.6 0.1 pad.3.clone
  45.7 0.0 copy-done
  45.7 0.6 constant_dynamic-slice_fusion.neighbours_ref
  46.3 0.7 maximum_maximum_fusion.table_ref
  47.0 2.7 %prepare.1 = (bf16[4,1024,128]{2,1,0:T(8,128)(2,1)}, f32[4,128]{1,0:T(4,128)}, f32[4,128,128]{2,1,0:T(8,128)}) custom-call(s32[1]{0:T(128)} %bitcast.zone_ref, s32[4,128]{1,0:T(4,128)} %constant_dynamic-slice_fusion.neighbours_ref, f32[8,1024]{1,0:T(8,128)} %maximum_maximum_fusion.table_ref, f32[32,32,128]{2,1,0:T(8,128)S(1)} %bitcast.15), custom_call_target="tpu_custom_call" | custom-call | tf_op jit(solution)/shard_map/prepare/pallas_call | solution.py:377
  49.6 11.7 %solve.1.transform_ref = f32[4,128,128]{2,1,0:T(8,128)} custom-call(bf16[4,1024,128]{2,1,0:T(8,128)(2,1)} %get-tuple-element.10.pick_ref, f32[4,128]{1,0:T(4,128)} %get-tuple-element.11.errors_ref, f32[4,128,128]{2,1,0:T(8,128)} %get-tuple-element.12.target_ref, f32[32,32,128]{2,1,0:T(8,128)S(1)} %all_to_all.20.readings_ref), custom_call_target="tpu_custom_call" | custom-call | tf_op jit(solution)/shard_map/solve/pallas_call | solution.py:392
  61.4 10.6 %all-to-all-done.2.cells_ref = f32[32,64,128]{2,1,0:T(8,128)S(1)} async-done(((f32[32,64,128]{2,1,0:T(8,128)}), f32[32,64,128]{2,1,0:T(8,128)S(1)}, u32[]{:S(2)}, u32[]{:S(2)}) %all-to-all-start.2) | async-done | bytes 1048608 | tf_op jit(solution)/shard_map/all_to_all | solution.py:372
  71.9 0.9 copy-done.1
  72.9 3.5 %analyse0.1 = f32[32,128,128]{2,1,0:T(8,128)} custom-call(s32[32]{0:T(128)} %counts_ref.1, f32[4,128,128]{2,1,0:T(8,128)S(1)} %copy-done.1, f32[32,64,128]{2,1,0:T(8,128)S(1)} %all-to-all-done.2.cells_ref), custom_call_target="tpu_custom_call" | custom-call | tf_op jit(solution)/shard_map/analyse0/pallas_call | solution.py:408
  76.3 3.1 %all-to-all-start.3 = ((f32[32,128,128]{2,1,0:T(8,128)}), f32[32,128,128]{2,1,0:T(8,128)S(1)}, u32[]{:S(2)}, u32[]{:S(2)}) async-start(f32[32,128,128]{2,1,0:T(8,128)} %analyse0.1), calls=%async_computation.3 | async-start | bytes 4194304 | tf_op jit(solution)/shard_map/all_to_all | solution.py:419
  79.5 0.6 dynamic_slice.6.count_ref
  80.1 47.7 %all-to-all-done.3.refs_0_ = f32[32,128,128]{2,1,0:T(8,128)S(1)} async-done(((f32[32,128,128]{2,1,0:T(8,128)}), f32[32,128,128]{2,1,0:T(8,128)S(1)}, u32[]{:S(2)}, u32[]{:S(2)}) %all-to-all-start.3) | async-done | bytes 2097184 | tf_op jit(solution)/shard_map/all_to_all | solution.py:419
  127.8 4.8 %advance.1 = f32[8,65536]{1,0:T(8,128)} custom-call(s32[1]{0:T(128)} %dynamic_slice.6.count_ref, f32[32,128,128]{2,1,0:T(8,128)S(1)} %all-to-all-done.3.refs_0_), custom_call_target="tpu_custom_call" | custom-call | tf_op jit(solution)/shard_map/advance/pallas_call | solution.py:422
  (7 shorter events, 0.0 us)
Async XLA Ops:
  0.0 45.7 %copy-start = (s32[128,128]{1,0:T(8,128)S(1)}, s32[128,128]{1,0:T(8,128)}, u32[]{:S(2)}) copy-start(s32[128,128]{1,0:T(8,128)} %param.11) | copy-start | bytes 196612
  1.7 22.4 %all-to-all-start = ((f32[32,4,1024]{2,1,0:T(4,128)}), f32[32,4,1024]{2,1,0:T(4,128)S(1)}, u32[]{:S(2)}, u32[]{:S(2)}) async-start(f32[32,4,1024]{2,1,0:T(4,128)} %broadcast_in_dim.10), calls=%async_computation | async-start | bytes 1048576 | tf_op jit(solution)/shard_map/all_to_all | solution.py:350
  8.8 36.9 %copy-start.2 = (s32[1024]{0:T(1024)S(1)}, s32[1024]{0:T(1024)}, u32[]{:S(2)}) copy-start(s32[1024]{0:T(1024)} %param.10) | copy-start | bytes 12292
  8.8 37.5 %copy-start.3 = (f32[1024]{0:T(1024)S(1)}, f32[1024]{0:T(1024)}, u32[]{:S(2)}) copy-start(f32[1024]{0:T(1024)} %param.9) | copy-start | bytes 12292
  8.8 37.5 %copy-start.4 = (f32[1024]{0:T(1024)S(1)}, f32[1024]{0:T(1024)}, u32[]{:S(2)}) copy-start(f32[1024]{0:T(1024)} %param.8) | copy-start | bytes 12292
  42.4 29.5 %all-to-all-start.2 = ((f32[32,64,128]{2,1,0:T(8,128)}), f32[32,64,128]{2,1,0:T(8,128)S(1)}, u32[]{:S(2)}, u32[]{:S(2)}) async-start(f32[32,64,128]{2,1,0:T(8,128)} %get-tuple-element.14), calls=%async_computation.2 | async-start | bytes 2097152 | tf_op jit(solution)/shard_map/all_to_all | solution.py:372
  71.9 1.0 copy-start.1
  76.3 3.2 %copy-start.5 = (s32[32]{0:T(128)S(1)}, s32[32]{0:T(128)}, u32[]{:S(2)}) copy-start(s32[32]{0:T(128)} %counts_ref.1) | copy-start | bytes 388
  76.3 51.5 %all-to-all-start.3 = ((f32[32,128,128]{2,1,0:T(8,128)}), f32[32,128,128]{2,1,0:T(8,128)S(1)}, u32[]{:S(2)}, u32[]{:S(2)}) async-start(f32[32,128,128]{2,1,0:T(8,128)} %analyse0.1), calls=%async_computation.3 | async-start | bytes 4194304 | tf_op jit(solution)/shard_map/all_to_all | solution.py:419
